TPU v7x, 128 devices: a whole 4x4x4 slice. The times are simulated.
128 devices in a mesh: seq: 32 (over y, z, core), batch: 4 (over x).
Axes of the slice: x: 4, y: 4, z: 4, core: 2. Of those that a mesh axis runs over, the one named last changes fastest.
Arguments:
- queries: bfloat16 [4, 4096, 4096], P('batch', 'seq'), may hold values from -130 to 130
- keys: bfloat16 [4, 4096, 1024], P('batch', 'seq'), may hold values from -4 to 4
- values: bfloat16 [4, 4096, 1024], P('batch', 'seq'), may hold values from -4 to 4
- lengths: int32 [4], P('batch'), may hold values from 2048 to 4096
- block_pos: int32 [4, 32], P('batch'), may hold values from 0 to 31, each once within a row
- w_in: bfloat16 [6144, 1024], replicated, may hold values from -0.078125 to 0.078125
- b_in: float32 [1024], replicated, may hold values from -3 to 3
- output_weight: bfloat16 [1024, 8], replicated, may hold values from -0.1875 to 0.1875
- output_bias: float32 [8], replicated, may hold values from 1 to 2
Outputs:
- grad_w_in: float32 [6144, 1024], P(('seq', 'batch'))
- grad_b_in: float32 [1024], replicated
- output_weight_gradient: float32 [1024, 8], replicated
- output_bias_gradient: float32 [8], replicated
Inputs may be any that keep to these rules, and one draw needn't show every extreme that they name: Each row of block_pos names every block 0 to 31 once.
All inputs are finite; a program needn't handle non-finite values.
Results may differ from a plain program's by a relative error of at most 0.0017.
The roundings to bfloat16 on the way count: a program that leaves them out, or rounds other values in their place, can miss the bound.
Values may be sent and summed in bfloat16 or wider, within the bound.
A program may use at most 128 MiB of HBM per device.

v0:
```python
import math

import jax
import jax.numpy as jnp
from jax import lax
from jax.sharding import PartitionSpec as P


def split_up(array, dim, size):
    before, after = (array.shape[:dim], array.shape[dim + 1 :])
    return jnp.moveaxis(array.reshape(*before, size, -1, *after), dim, 0)


def sent_and_summed(array, axis, dim):
    size = lax.axis_size(axis)
    tiles = lax.all_to_all(split_up(array, dim, size), axis, 0, 0, tiled=True)
    return jnp.sum(tiles, axis=0)


def in_one(arrays, axis):
    ends = [0]
    for a in arrays:
        ends.append(ends[-1] + a.size)
    so_far = lax.psum(jnp.concatenate([a.ravel() for a in arrays]), axis)
    return tuple((so_far[b:e].reshape(a.shape) for a, b, e in zip(arrays, ends, ends[1:])))


def on_device(queries, keys, values, lengths, block_pos, w_in, b_in, output_weight, output_bias):
    q_rows = queries[0]
    k_rows = keys[0]
    v_rows = values[0]
    rows = q_rows.shape[0]
    heads_kv = output_weight.shape[1]
    head_size = k_rows.shape[1] // heads_kv
    group_index = q_rows.shape[1] // k_rows.shape[1]
    scale = 1.0 / math.sqrt(head_size)
    every_key = lax.all_gather(k_rows, "seq", axis=0, tiled=True)
    total = every_key.shape[0]
    order = block_pos[0]
    offsets = jnp.arange(rows, dtype=jnp.int32)
    key_pos = (order[:, None] * rows + offsets[None, :]).reshape(-1)
    mine = lax.axis_index("seq")
    query_pos = lax.dynamic_index_in_dim(order, mine, 0, keepdims=False) * rows + offsets
    limit = lengths[0]
    allowed = (key_pos[None, :] <= query_pos[:, None]) & (key_pos < limit)[None, :]
    query_live = (query_pos < limit).astype(jnp.float32)

    def group_mass(index, sums):
        q_part = lax.dynamic_slice_in_dim(
            q_rows, index * group_index * head_size, group_index * head_size, 1
        )
        q_part = q_part.reshape(rows, group_index, head_size)
        k_part = lax.dynamic_slice_in_dim(every_key, index * head_size, head_size, 1)
        scores = (
            jnp.einsum("qhd,kd->hqk", q_part, k_part, preferred_element_type=jnp.float32) * scale
        )
        masked = jnp.where(allowed[None], scores, -1e30)
        top = jnp.max(masked, axis=2, keepdims=True)
        weights = jnp.where(allowed[None], jnp.exp(masked - top), 0.0)
        denom = jnp.sum(weights, axis=2, keepdims=True)
        share = weights / denom * query_live[None, :, None]
        column = jnp.sum(share, axis=(0, 1))
        return lax.dynamic_update_index_in_dim(sums, column, index, 0)

    partial_value = lax.fori_loop(
        0, heads_kv, group_mass, jnp.zeros((heads_kv, total), jnp.float32)
    )
    mass = sent_and_summed(partial_value, "seq", 1)
    labels = jnp.log1p(mass).T
    features = jnp.concatenate([q_rows, k_rows, v_rows], axis=1)
    pre = jnp.dot(features, w_in, preferred_element_type=jnp.float32) + b_in
    act = jax.nn.silu(pre).astype(jnp.bfloat16)
    pred = jnp.dot(act, output_weight, preferred_element_type=jnp.float32) + output_bias
    norm = 1.0 / math.sqrt(lax.axis_size("batch") * total)
    resid = ((pred - labels) * query_live[:, None] * norm).astype(jnp.bfloat16)
    back = lax.dot_general(
        resid, output_weight, (((1,), (1,)), ((), ())), preferred_element_type=jnp.float32
    )
    sig = jax.nn.sigmoid(pre)
    delta = (back * sig * (1.0 + pre * (1.0 - sig))).astype(jnp.bfloat16)
    out_term = lax.dot_general(
        act, resid, (((0,), (0,)), ((), ())), preferred_element_type=jnp.float32
    )
    grad_b_in, output_weight_gradient, output_bias_gradient = in_one(
        (
            jnp.sum(delta.astype(jnp.float32), axis=0),
            out_term,
            jnp.sum(resid.astype(jnp.float32), axis=0),
        ),
        ("seq", "batch"),
    )
    grad_w_in = lax.psum_scatter(
        lax.dot_general(
            features, delta, (((0,), (0,)), ((), ())), preferred_element_type=jnp.float32
        ),
        ("seq", "batch"),
        scatter_dimension=0,
        tiled=True,
    )
    return (grad_w_in, grad_b_in, output_weight_gradient, output_bias_gradient)


def solution(mesh):
    return jax.shard_map(
        on_device,
        mesh=mesh,
        in_specs=(
            P("batch", "seq", None),
            P("batch", "seq", None),
            P("batch", "seq", None),
            P("batch"),
            P("batch", None),
            P(),
            P(),
            P(),
            P(),
        ),
        out_specs=(P(("seq", "batch"), None), P(), P(), P()),
        check_vma=False,
    )
```

profile of v0, /device:TPU:1, one launch (start us, length us, event | category | flops | bytes accessed | tf_op | source)
XLA Modules:
  0.0 517.5 jit_solution(12301234503528148574)
XLA Ops:
  7.2 0.7 all-gather.3.cloned.1.call-update
  7.9 1.1 copy.15
  9.7 1.1 copy.16
  10.8 1.6 copy.14
  12.5 1.2 fusion.51
  13.7 0.6 iota_add_fusion
  14.4 0.7 multiply_bitcast_fusion
  15.2 51.6 %all-gather.3.cloned.1.call-done = bf16[1,4096,1024]{2,1,0:T(8,128)(2,1)} async-done(((bf16[1,128,1024]{2,1,0:T(8,128)(2,1)}), bf16[1,4096,1024]{2,1,0:T(8,128)(2,1)}) %all-gather.3.cloned.1.call-update) | async-done | bytes 8388624 | tf_op jit(solution)/shard_map/all_gather | solution.py:37
  66.8 170.6 %while.16 = (s32[]{:T(128)}, f32[8,4096]{1,0:T(8,128)}, bf16[4096,1024]{1,0:T(8,128)(2,1)}, bf16[128,4096]{0,1:T(8,128)(2,1)S(1)}, s32[128]{0:T(128)S(1)}, /*ind...) while((s32[]{:T(128)}, f32[8,4096]{1,0:T(8,128)}, ...), condition=%wide.region_4.5_spmd.clone, body=%wide.region_0.4_spmd.clone.sunk | while | flops 1097869184 | bytes 22091528 | solution.py:65
  66.8 1.3 compare_convert_fusion.3
  68.1 1.4 compare_and_fusion.2
  69.5 8.6 %fusion.72 = f32[4,128,4096]{1,2,0:T(8,128)} fusion(pred[128,4096]{0,1:T(8,128)(4,1)S(1)} %compare_and_fusion.2, bf16[128,4,128]{0,2,1:T(8,128)(2,1)S(1)} %bitcast.69, bf16[4096,1024]{1,0:T(8,128)(2,1)} %get-tuple-element.300, s32[]{:T(128)S(6)} %select_n.79), kind=kOutput, calls=%fused_computation.2.clone.1 | convolution fusion | flops 545268736 | bytes 10616836 | tf_op jit(solution)/shard_map/while/body/eval_jaxpr/div | solution.py:61
  78.1 8.4 %multiply_reduce_fusion.2 = f32[4096]{0:T(1024)S(1)} fusion(f32[4,128,4096]{1,2,0:T(8,128)} %fusion.72, f32[128]{0:T(128)S(1)} %compare_convert_fusion.3, pred[128,4096]{0,1:T(8,128)(4,1)S(1)} %compare_and_fusion.2, bf16[128,4,128]{0,2,1:T(8,128)(2,1)S(1)} %bitcast.70, bf16[4096,1024]{1,0:T(8,128)(2,1)} %get-tuple-element.300, s32[]{:T(128)S(6)} %select_n.79), kind=kOutput, calls=%fused_computation.5.clone.1 | convolution fusion | flops 551551488 | bytes 10633732 | tf_op jit(solution)/shard_map/while/body/eval_jaxpr/sub | solution.py:59
  86.5 1.6 dynamic_update_slice.13
  88.1 1.3 compare_convert_fusion.3
  89.4 1.4 compare_and_fusion.2
  90.8 8.6 %fusion.72 = f32[4,128,4096]{1,2,0:T(8,128)} fusion(pred[128,4096]{0,1:T(8,128)(4,1)S(1)} %compare_and_fusion.2, bf16[128,4,128]{0,2,1:T(8,128)(2,1)S(1)} %bitcast.69, bf16[4096,1024]{1,0:T(8,128)(2,1)} %get-tuple-element.300, s32[]{:T(128)S(6)} %select_n.79), kind=kOutput, calls=%fused_computation.2.clone.1 | convolution fusion | flops 545268736 | bytes 10616836 | tf_op jit(solution)/shard_map/while/body/eval_jaxpr/div | solution.py:61
  99.4 8.4 %multiply_reduce_fusion.2 = f32[4096]{0:T(1024)S(1)} fusion(f32[4,128,4096]{1,2,0:T(8,128)} %fusion.72, f32[128]{0:T(128)S(1)} %compare_convert_fusion.3, pred[128,4096]{0,1:T(8,128)(4,1)S(1)} %compare_and_fusion.2, bf16[128,4,128]{0,2,1:T(8,128)(2,1)S(1)} %bitcast.70, bf16[4096,1024]{1,0:T(8,128)(2,1)} %get-tuple-element.300, s32[]{:T(128)S(6)} %select_n.79), kind=kOutput, calls=%fused_computation.5.clone.1 | convolution fusion | flops 551551488 | bytes 10633732 | tf_op jit(solution)/shard_map/while/body/eval_jaxpr/sub | solution.py:59
  107.8 1.6 dynamic_update_slice.13
  109.4 1.3 compare_convert_fusion.3
  110.8 1.4 compare_and_fusion.2
  112.2 8.6 %fusion.72 = f32[4,128,4096]{1,2,0:T(8,128)} fusion(pred[128,4096]{0,1:T(8,128)(4,1)S(1)} %compare_and_fusion.2, bf16[128,4,128]{0,2,1:T(8,128)(2,1)S(1)} %bitcast.69, bf16[4096,1024]{1,0:T(8,128)(2,1)} %get-tuple-element.300, s32[]{:T(128)S(6)} %select_n.79), kind=kOutput, calls=%fused_computation.2.clone.1 | convolution fusion | flops 545268736 | bytes 10616836 | tf_op jit(solution)/shard_map/while/body/eval_jaxpr/div | solution.py:61
  120.8 8.4 %multiply_reduce_fusion.2 = f32[4096]{0:T(1024)S(1)} fusion(f32[4,128,4096]{1,2,0:T(8,128)} %fusion.72, f32[128]{0:T(128)S(1)} %compare_convert_fusion.3, pred[128,4096]{0,1:T(8,128)(4,1)S(1)} %compare_and_fusion.2, bf16[128,4,128]{0,2,1:T(8,128)(2,1)S(1)} %bitcast.70, bf16[4096,1024]{1,0:T(8,128)(2,1)} %get-tuple-element.300, s32[]{:T(128)S(6)} %select_n.79), kind=kOutput, calls=%fused_computation.5.clone.1 | convolution fusion | flops 551551488 | bytes 10633732 | tf_op jit(solution)/shard_map/while/body/eval_jaxpr/sub | solution.py:59
  129.1 1.6 dynamic_update_slice.13
  130.7 1.3 compare_convert_fusion.3
  132.1 1.4 compare_and_fusion.2
  133.5 8.6 %fusion.72 = f32[4,128,4096]{1,2,0:T(8,128)} fusion(pred[128,4096]{0,1:T(8,128)(4,1)S(1)} %compare_and_fusion.2, bf16[128,4,128]{0,2,1:T(8,128)(2,1)S(1)} %bitcast.69, bf16[4096,1024]{1,0:T(8,128)(2,1)} %get-tuple-element.300, s32[]{:T(128)S(6)} %select_n.79), kind=kOutput, calls=%fused_computation.2.clone.1 | convolution fusion | flops 545268736 | bytes 10616836 | tf_op jit(solution)/shard_map/while/body/eval_jaxpr/div | solution.py:61
  142.1 8.4 %multiply_reduce_fusion.2 = f32[4096]{0:T(1024)S(1)} fusion(f32[4,128,4096]{1,2,0:T(8,128)} %fusion.72, f32[128]{0:T(128)S(1)} %compare_convert_fusion.3, pred[128,4096]{0,1:T(8,128)(4,1)S(1)} %compare_and_fusion.2, bf16[128,4,128]{0,2,1:T(8,128)(2,1)S(1)} %bitcast.70, bf16[4096,1024]{1,0:T(8,128)(2,1)} %get-tuple-element.300, s32[]{:T(128)S(6)} %select_n.79), kind=kOutput, calls=%fused_computation.5.clone.1 | convolution fusion | flops 551551488 | bytes 10633732 | tf_op jit(solution)/shard_map/while/body/eval_jaxpr/sub | solution.py:59
  150.5 1.6 dynamic_update_slice.13
  152.1 1.3 compare_convert_fusion.3
  153.4 1.4 compare_and_fusion.2
  154.8 8.6 %fusion.72 = f32[4,128,4096]{1,2,0:T(8,128)} fusion(pred[128,4096]{0,1:T(8,128)(4,1)S(1)} %compare_and_fusion.2, bf16[128,4,128]{0,2,1:T(8,128)(2,1)S(1)} %bitcast.69, bf16[4096,1024]{1,0:T(8,128)(2,1)} %get-tuple-element.300, s32[]{:T(128)S(6)} %select_n.79), kind=kOutput, calls=%fused_computation.2.clone.1 | convolution fusion | flops 545268736 | bytes 10616836 | tf_op jit(solution)/shard_map/while/body/eval_jaxpr/div | solution.py:61
  163.4 8.4 %multiply_reduce_fusion.2 = f32[4096]{0:T(1024)S(1)} fusion(f32[4,128,4096]{1,2,0:T(8,128)} %fusion.72, f32[128]{0:T(128)S(1)} %compare_convert_fusion.3, pred[128,4096]{0,1:T(8,128)(4,1)S(1)} %compare_and_fusion.2, bf16[128,4,128]{0,2,1:T(8,128)(2,1)S(1)} %bitcast.70, bf16[4096,1024]{1,0:T(8,128)(2,1)} %get-tuple-element.300, s32[]{:T(128)S(6)} %select_n.79), kind=kOutput, calls=%fused_computation.5.clone.1 | convolution fusion | flops 551551488 | bytes 10633732 | tf_op jit(solution)/shard_map/while/body/eval_jaxpr/sub | solution.py:59
  171.8 1.6 dynamic_update_slice.13
  173.4 1.3 compare_convert_fusion.3
  174.7 1.4 compare_and_fusion.2
  176.1 8.6 %fusion.72 = f32[4,128,4096]{1,2,0:T(8,128)} fusion(pred[128,4096]{0,1:T(8,128)(4,1)S(1)} %compare_and_fusion.2, bf16[128,4,128]{0,2,1:T(8,128)(2,1)S(1)} %bitcast.69, bf16[4096,1024]{1,0:T(8,128)(2,1)} %get-tuple-element.300, s32[]{:T(128)S(6)} %select_n.79), kind=kOutput, calls=%fused_computation.2.clone.1 | convolution fusion | flops 545268736 | bytes 10616836 | tf_op jit(solution)/shard_map/while/body/eval_jaxpr/div | solution.py:61
  184.7 8.4 %multiply_reduce_fusion.2 = f32[4096]{0:T(1024)S(1)} fusion(f32[4,128,4096]{1,2,0:T(8,128)} %fusion.72, f32[128]{0:T(128)S(1)} %compare_convert_fusion.3, pred[128,4096]{0,1:T(8,128)(4,1)S(1)} %compare_and_fusion.2, bf16[128,4,128]{0,2,1:T(8,128)(2,1)S(1)} %bitcast.70, bf16[4096,1024]{1,0:T(8,128)(2,1)} %get-tuple-element.300, s32[]{:T(128)S(6)} %select_n.79), kind=kOutput, calls=%fused_computation.5.clone.1 | convolution fusion | flops 551551488 | bytes 10633732 | tf_op jit(solution)/shard_map/while/body/eval_jaxpr/sub | solution.py:59
  193.1 1.6 dynamic_update_slice.13
  194.7 1.3 compare_convert_fusion.3
  196.0 1.4 compare_and_fusion.2
  197.4 8.6 %fusion.72 = f32[4,128,4096]{1,2,0:T(8,128)} fusion(pred[128,4096]{0,1:T(8,128)(4,1)S(1)} %compare_and_fusion.2, bf16[128,4,128]{0,2,1:T(8,128)(2,1)S(1)} %bitcast.69, bf16[4096,1024]{1,0:T(8,128)(2,1)} %get-tuple-element.300, s32[]{:T(128)S(6)} %select_n.79), kind=kOutput, calls=%fused_computation.2.clone.1 | convolution fusion | flops 545268736 | bytes 10616836 | tf_op jit(solution)/shard_map/while/body/eval_jaxpr/div | solution.py:61
  206.0 8.4 %multiply_reduce_fusion.2 = f32[4096]{0:T(1024)S(1)} fusion(f32[4,128,4096]{1,2,0:T(8,128)} %fusion.72, f32[128]{0:T(128)S(1)} %compare_convert_fusion.3, pred[128,4096]{0,1:T(8,128)(4,1)S(1)} %compare_and_fusion.2, bf16[128,4,128]{0,2,1:T(8,128)(2,1)S(1)} %bitcast.70, bf16[4096,1024]{1,0:T(8,128)(2,1)} %get-tuple-element.300, s32[]{:T(128)S(6)} %select_n.79), kind=kOutput, calls=%fused_computation.5.clone.1 | convolution fusion | flops 551551488 | bytes 10633732 | tf_op jit(solution)/shard_map/while/body/eval_jaxpr/sub | solution.py:59
  214.4 1.6 dynamic_update_slice.13
  216.0 1.3 compare_convert_fusion.3
  217.4 1.4 compare_and_fusion.2
  218.8 8.6 %fusion.72 = f32[4,128,4096]{1,2,0:T(8,128)} fusion(pred[128,4096]{0,1:T(8,128)(4,1)S(1)} %compare_and_fusion.2, bf16[128,4,128]{0,2,1:T(8,128)(2,1)S(1)} %bitcast.69, bf16[4096,1024]{1,0:T(8,128)(2,1)} %get-tuple-element.300, s32[]{:T(128)S(6)} %select_n.79), kind=kOutput, calls=%fused_computation.2.clone.1 | convolution fusion | flops 545268736 | bytes 10616836 | tf_op jit(solution)/shard_map/while/body/eval_jaxpr/div | solution.py:61
  227.4 8.4 %multiply_reduce_fusion.2 = f32[4096]{0:T(1024)S(1)} fusion(f32[4,128,4096]{1,2,0:T(8,128)} %fusion.72, f32[128]{0:T(128)S(1)} %compare_convert_fusion.3, pred[128,4096]{0,1:T(8,128)(4,1)S(1)} %compare_and_fusion.2, bf16[128,4,128]{0,2,1:T(8,128)(2,1)S(1)} %bitcast.70, bf16[4096,1024]{1,0:T(8,128)(2,1)} %get-tuple-element.300, s32[]{:T(128)S(6)} %select_n.79), kind=kOutput, calls=%fused_computation.5.clone.1 | convolution fusion | flops 551551488 | bytes 10633732 | tf_op jit(solution)/shard_map/while/body/eval_jaxpr/sub | solution.py:59
  235.7 1.6 dynamic_update_slice.13
  237.4 5.5 %all-to-all-start = ((f32[32,8,128]{2,1,0:T(8,128)}), f32[32,8,128]{2,1,0:T(8,128)S(1)}, u32[]{:S(2)}, u32[]{:S(2)}) async-start(f32[32,8,128]{2,1,0:T(8,128)} %bitcast.9), calls=%async_computation | async-start | bytes 262144 | tf_op jit(solution)/shard_map/all_to_all | solution.py:16
  243.1 6.5 %multiply_convert_fusion = (bf16[128,1024]{1,0:T(8,128)(2,1)S(1)}, f32[128,1024]{1,0:T(8,128)S(1)}) fusion(f32[1024]{0:T(1024)S(1)} %copy-done.1, bf16[6144,1024]{1,0:T(8,128)(2,1)} %param.16, bf16[128,1024]{0,1:T(8,128)(2,1)S(1)} %bitcast.73, bf16[128,1024]{0,1:T(8,128)(2,1)S(1)} %bitcast.71, bf16[128,4096]{0,1:T(8,128)(2,1)S(1)} %get-tuple-element.317), kind=kOutput, calls=%fused_computation.42 | convolution fusion | flops 1616117760 | bytes 14946304 | tf_op jit(solution)/shard_map/dot_general | solution.py:71
  249.6 0.7 compare_convert_fusion.1
  250.3 0.3 all-to-all-done
  250.6 0.3 convert_reduce_fusion.1
  250.9 0.4 convert_reduce_fusion
  251.3 13.2 %fusion.46 = f32[6144,1024]{1,0:T(8,128)} fusion(bf16[128,1024]{1,0:T(8,128)(2,1)S(1)} %get-tuple-element.212, bf16[128,1024]{0,1:T(8,128)(2,1)S(1)} %bitcast.74, bf16[128,1024]{0,1:T(8,128)(2,1)S(1)} %bitcast.72, bf16[128,4096]{0,1:T(8,128)(2,1)S(1)} %get-tuple-element.317), kind=kOutput, calls=%fused_computation.40 | convolution fusion | flops 1615331328 | bytes 27000832 | tf_op jit(solution)/shard_map/dot_general | solution.py:93
  264.5 0.3 fusion.52
  264.8 0.3 reshape.87
  265.0 66.5 %psum.7 = f32[9224]{0:T(1024)S(1)} all-reduce(f32[9224]{0:T(1024)S(1)} %pad_maximum_fusion.3), channel_id=1, replica_groups=mesh['seq'=32,'batch'=4] {'seq','batch'}, use_global_device_ids=true, to_apply=%region_9.10 | all-reduce | flops 9224 | bytes 73792 | tf_op jit(solution)/shard_map/psum | solution.py:24
  331.5 0.5 slice.22
  332.1 0.6 slice.20
  332.6 0.3 reshape.88
  332.9 0.8 copy.18
  333.7 176.9 %reduce-scatter.2.cloned.1.call-done = f32[48,1024]{1,0:T(8,128)} async-done(((f32[6144,1024]{1,0:T(8,128)}), f32[48,1024]{1,0:T(8,128)}) %reduce-scatter.2.cloned.1.call-update) | async-done | bytes 196624 | tf_op jit(solution)/shard_map/reduce_scatter | solution.py:92
  (23 shorter events, 0.6 us)
Async XLA Ops:
  7.2 243.4 %copy-start = (bf16[1024,8]{0,1:T(8,128)(2,1)S(1)}, bf16[1024,8]{0,1:T(8,128)(2,1)}, u32[]{:S(2)}) copy-start(bf16[1024,8]{0,1:T(8,128)(2,1)} %param.18) | copy-start | bytes 49156
  7.2 59.6 %all-gather.3.cloned.1.call-start = ((), (), s32[]{:S(2)}) async-start(), calls=%async_computation.3 | async-start | bytes 8650752 | tf_op jit(solution)/shard_map/all_gather | solution.py:37
  66.8 176.4 %copy-start.1 = (f32[1024]{0:T(1024)S(1)}, f32[1024]{0:T(1024)}, u32[]{:S(2)}) copy-start(f32[1024]{0:T(1024)} %param.17) | copy-start | bytes 12292
  237.4 13.2 %all-to-all-start = ((f32[32,8,128]{2,1,0:T(8,128)}), f32[32,8,128]{2,1,0:T(8,128)S(1)}, u32[]{:S(2)}, u32[]{:S(2)}) async-start(f32[32,8,128]{2,1,0:T(8,128)} %bitcast.9), calls=%async_computation | async-start | bytes 262144 | tf_op jit(solution)/shard_map/all_to_all | solution.py:16
  242.9 267.8 %reduce-scatter.2.cloned.1.call-start = ((), (), s32[]{:S(2)}) async-start(), calls=%async_computation.2 | async-start | bytes 25362432 | tf_op jit(solution)/shard_map/reduce_scatter | solution.py:92
  243.1 7.5 %copy-start.2 = (f32[8]{0:T(128)S(1)}, f32[8]{0:T(128)}, u32[]{:S(2)}) copy-start(f32[8]{0:T(128)} %param.19) | copy-start | bytes 100
Sparse Core Ops, SparseCore 0:
  10.3 56.4 all-gather.2
  264.6 245.9 reduce-scatter.1
where the time goes:
time: 520 us; the launch traced here: 518 us
  waiting for transfers between devices  229 us (44%)
  matrix products  156 us (30%)
  blocking collectives  66.5 us (13%)
  other arithmetic  24.9 us (5%)
  local copies, waits for them, and re-layouts  19.4 us (4%)
  between operations  14.8 us (3%)
  starting transfers between devices  5.78 us (1%)
    reduce_scatter x1, waiting for transfers between devices, on_device(): lax.psum_scatter(lax.dot_general(features, delta, (((0,), (0,)), ((), ())...  177 us
    div x8, matrix products, group_mass(): share = weights / denom * query_live[None, :, None]  68.8 us
    sub x8, matrix products, group_mass(): weights = jnp.where(allowed[None], jnp.exp(masked - top), 0.0)  67 us
    psum x1, blocking collectives, in_one(): so_far = lax.psum(jnp.concatenate([a.ravel() for a in arrays]), axis)  66.5 us
    all_gather x1, waiting for transfers between devices, on_device(): every_key = lax.all_gather(k_rows, 'seq', axis=0, tiled=True)  51.6 us
    dot_general x1, matrix products, on_device(): lax.dot_general(features, delta, (((0,), (0,)), ((), ())), preferred_elem...  13.2 us
    dynamic_update_slice x8, local copies, waits for them, and re-layouts, group_mass(): return lax.dynamic_update_index_in_dim(sums, column, index, 0)  12.9 us
    and x8, other arithmetic, on_device(): (key_pos[None, :] <= query_pos[:, None]) & (key_pos < limit)[None, :]  11.1 us
  transfers between devices with their start and end apart: 3, of which 3 were waited for; matrix products, arithmetic and copies ran while one was open for 3% of the time, Pallas kernels for 0%

commit v1 on v0

v1 whole, which is shorter than its diff:
```python
import functools
import math

import jax
import jax.numpy as jnp
from jax import lax
from jax.experimental import pallas as pl
from jax.experimental.pallas import tpu as pltpu
from jax.sharding import PartitionSpec as P

MESH = pl.DeviceIdType.MESH
F32 = jnp.float32
BF16 = jnp.bfloat16
VM = pltpu.VMEM
CK = 512
WK = 512


def place():
    seq = lax.axis_index("seq")
    x = lax.axis_index("batch")
    y = seq // 8
    row = lax.rem(seq, 8)
    core = lax.rem(seq, 2)
    return seq, x, y, row, core


def greet(seq, x, y, row, core):
    bar = pltpu.get_barrier_semaphore()
    n = 0
    for k in range(1, 8):
        pl.semaphore_signal(
            bar, inc=1, device_id=(y * 8 + lax.rem(row + k, 8), x), device_id_type=MESH
        )
        n += 1
    for k in range(1, 4):
        pl.semaphore_signal(
            bar, inc=1, device_id=(lax.rem(y + k, 4) * 8 + row, x), device_id_type=MESH
        )
        n += 1
    for k in range(1, 8):
        pl.semaphore_signal(bar, inc=1, device_id=group_peer(seq, x, core, k), device_id_type=MESH)
        n += 1
    pl.semaphore_wait(bar, n)


def group_rank(x, core):
    return core * 4 + x


def group_peer(seq, x, core, k):
    j = lax.rem(group_rank(x, core) + k, 8)
    return (seq - core + j // 4, lax.rem(j, 4))


def remote(src, dst, ss, rs, dev):
    return pltpu.make_async_remote_copy(
        src_ref=src, dst_ref=dst, send_sem=ss, recv_sem=rs, device_id=dev, device_id_type=MESH
    )


def spread_kernel(
    q, k, v, w_hbm, b_in, wo, bo, qg, kg, ft_all, sp, act, pred,
    ft, wbuf, pre, wsem, ks, kr, qs, qr, fs, fr, ys, yr, ls,
):
    seq, x, y, row, core = place()
    j = group_rank(x, core)
    chunks = w_hbm.shape[0] // WK

    def fetch(i):
        return pltpu.make_async_copy(
            w_hbm.at[pl.ds(i * WK, WK)], wbuf.at[i % 3], wsem.at[i % 3]
        )

    fetch(0).start()
    fetch(1).start()
    greet(seq, x, y, row, core)
    kc, qc, fc, yc = [], [], [], []
    for n in range(1, 8):
        to = lax.rem(row + n, 8)
        c = remote(
            k.at[:, pl.ds(pl.multiple_of(to * 128, 128), 128)], kg.at[seq],
            ks.at[n], kr.at[n], (y * 8 + to, x),
        )
        c.start()
        kc.append(c)
    for n in range(1, 8):
        to = lax.rem(row + n, 8)
        c = remote(
            q.at[:, pl.ds(pl.multiple_of(to * 512, 512), 512)], qg.at[row],
            qs.at[n], qr.at[n], (y * 8 + to, x),
        )
        c.start()
        qc.append(c)
    own_k = pltpu.make_async_copy(
        k.at[:, pl.ds(pl.multiple_of(row * 128, 128), 128)], kg.at[seq], ls.at[0]
    )
    own_q = pltpu.make_async_copy(
        q.at[:, pl.ds(pl.multiple_of(row * 512, 512), 512)], qg.at[row], ls.at[1]
    )
    own_k.start()
    own_q.start()
    for i in range(16):
        src, lo = (q, i * 384)
        parts = []
        for t in range(3):
            col = lo + t * 128
            if col < 4096:
                parts.append(q[:, col : col + 128])
            elif col < 5120:
                parts.append(k[:, col - 4096 : col - 3968])
            else:
                parts.append(v[:, col - 5120 : col - 4992])
        block = jnp.concatenate(parts, axis=1).astype(F32).T.astype(BF16)
        for t in range(8):
            ft[i, t] = block[t * 48 : (t + 1) * 48]
    lanes = pl.ds(pl.multiple_of(j * 128, 128), 128)
    for n in range(1, 8):
        to = lax.rem(j + n, 8)
        c = remote(
            ft.at[:, to], ft_all.at[:, :, lanes], fs.at[n], fr.at[n], group_peer(seq, x, core, n)
        )
        c.start()
        fc.append(c)
    own_f = pltpu.make_async_copy(ft.at[:, j], ft_all.at[:, :, lanes], ls.at[2])
    own_f.start()

    def multiply(i):
        if i + 2 < chunks:
            fetch(i + 2).start()
        fetch(i).wait()
        lo = i * WK
        if lo < 4096:
            a = q[:, lo : lo + WK]
        elif lo < 5120:
            a = k[:, lo - 4096 : lo - 4096 + WK]
        else:
            a = v[:, lo - 5120 : lo - 5120 + WK]
        part = jnp.dot(a, wbuf[i % 3], preferred_element_type=F32)
        pre[...] = part if i == 0 else pre[...] + part

    for i in range(chunks // 2):
        multiply(i)
    for c in kc:
        c.wait()
    own_k.wait()
    mine = kg.at[pl.ds(y * 8, 8)]
    for n in range(1, 4):
        c = remote(mine, mine, ys.at[n], yr.at[n], (lax.rem(y + n, 4) * 8 + row, x))
        c.start()
        yc.append(c)
    for i in range(chunks // 2, chunks):
        multiply(i)
    z = pre[...] + b_in[...]
    sig = jax.nn.sigmoid(z)
    a = (z * sig).astype(BF16)
    act[...] = a
    sp[...] = sig * (1.0 + z * (1.0 - sig))
    pred[...] = lax.dot_general(
        wo[...], a, (((1,), (1,)), ((), ())), preferred_element_type=F32
    )[0:8] + bo[...]
    for c in qc + fc + yc:
        c.wait()
    own_q.wait()
    own_f.wait()


def spread(q, k, v, w, b_in, wo, bo):
    dma = pltpu.SemaphoreType.DMA
    vmem = pl.BlockSpec(memory_space=VM)
    return pl.pallas_call(
        spread_kernel,
        name="spread",
        out_shape=(
            jax.ShapeDtypeStruct((8, 128, 512), BF16),
            jax.ShapeDtypeStruct((32, 128, 128), BF16),
            jax.ShapeDtypeStruct((16, 48, 1024), BF16),
            jax.ShapeDtypeStruct((128, 1024), F32),
            jax.ShapeDtypeStruct((128, 1024), BF16),
            jax.ShapeDtypeStruct((8, 128), F32),
        ),
        in_specs=[vmem, vmem, vmem, pl.BlockSpec(memory_space=pl.ANY), vmem, vmem, vmem],
        out_specs=(vmem,) * 6,
        scratch_shapes=[
            VM((16, 8, 48, 128), BF16),
            VM((3, WK, 1024), BF16),
            VM((128, 1024), F32),
            dma((3,)),
            dma((8,)), dma((8,)), dma((8,)), dma((8,)), dma((8,)), dma((8,)), dma((4,)), dma((4,)),
            dma((3,)),
        ],
        compiler_params=pltpu.CompilerParams(
            collective_id=0, has_side_effects=True, vmem_limit_bytes=48 * 2**20
        ),
    )(q, k, v, w, b_in, wo, bo)


def mass_kernel(meta, qg, kg, out, kpos, s_ref, acc):
    limit = meta[32]
    first = meta[33]
    factor = math.log2(math.e) / math.sqrt(128)

    def order(r, _):
        kpos[pl.ds(pl.multiple_of(meta[r] * 128, 128), 128)] = kg[r]
        return 0

    lax.fori_loop(0, 32, order, 0)
    acc[...] = jnp.zeros_like(acc)
    lane = lax.rem(lax.broadcasted_iota(jnp.int32, (1, 512), 1), 128)
    sub = lax.broadcasted_iota(jnp.int32, (CK, 512), 0)

    def fold(a, op):
        return op(a.reshape(CK // 8, 8, 512), axis=0)

    def block(i, _):
        pos = meta[first + i]

        @pl.when(pos * 128 < limit)
        def _():
            last = pos * 128 // CK
            q4 = jnp.concatenate([qg[i, :, h * 128 : (h + 1) * 128] for h in range(4)], axis=0)

            def scores(c):
                rows = pl.ds(pl.multiple_of(c * CK, CK), CK)
                return rows, lax.dot_general(
                    kpos[rows], q4, (((1,), (1,)), ((), ())), preferred_element_type=F32
                )

            def first_pass(c, top):
                rows, s = scores(c)
                s_ref[rows] = s
                return jnp.maximum(top, fold(s, jnp.max))

            top = lax.fori_loop(0, last, first_pass, jnp.full((8, 512), -1e30, F32))
            rows, s = scores(last)
            s = jnp.where(sub + last * CK <= lane + pos * 128, s, -1e30)
            s_ref[rows] = s
            top = jnp.max(jnp.maximum(top, fold(s, jnp.max)), axis=0, keepdims=True)

            def second_pass(c, total):
                rows = pl.ds(pl.multiple_of(c * CK, CK), CK)
                e = jnp.exp2((s_ref[rows] - top) * factor)
                s_ref[rows] = e
                return total + fold(e, jnp.sum)

            total = lax.fori_loop(0, last + 1, second_pass, jnp.zeros((8, 512), F32))
            total = jnp.sum(total, axis=0, keepdims=True)
            share = jnp.where(lane + pos * 128 < limit, 1.0 / total, 0.0)

            def third_pass(c, _):
                rows = pl.ds(pl.multiple_of(c * CK, CK), CK)
                e = s_ref[rows] * share
                acc[rows] += (e[:, 0:128] + e[:, 128:256]) + (e[:, 256:384] + e[:, 384:512])
                return 0

            lax.fori_loop(0, last + 1, third_pass, 0)

        return 0

    lax.fori_loop(0, 8, block, 0)

    def give(r, _):
        rows = acc[pl.ds(pl.multiple_of(meta[r] * 128, 128), 128)]
        out[pl.ds(r, 1)] = jnp.sum(rows.T, axis=0, keepdims=True)
        return 0

    lax.fori_loop(0, 32, give, 0)


def column_mass(meta, qg, kg):
    vmem = pl.BlockSpec(memory_space=VM)
    return pl.pallas_call(
        mass_kernel,
        name="column_mass",
        out_shape=jax.ShapeDtypeStruct((32, 128), F32),
        in_specs=[pl.BlockSpec(memory_space=pltpu.SMEM), vmem, vmem],
        out_specs=vmem,
        scratch_shapes=[VM((4096, 128), BF16), VM((4096, 512), F32), VM((4096, 128), F32)],
        compiler_params=pltpu.CompilerParams(vmem_limit_bytes=48 * 2**20),
    )(meta, qg, kg)


def reduce_kernel(
    norm, mass, sp, act, pred, live, wo, ft, out, small,
    m1, m2s, m2, dl, ga, gb, own_a, own_b, ra, rb, pa, pb, ta, tb,
    pk, p1, p2, p3,
    s1, r1, s2, r2, s3, r3, s4, r4, s5, r5, sa, qa, sb, qb, s6, r6, s7, r7, s8, r8, s9, r9,
):
    seq, x, y, row, core = place()
    z = row // 2
    j = group_rank(x, core)
    greet(seq, x, y, row, core)

    def y_dev(n):
        return (lax.rem(y + n, 4) * 8 + row, x)

    def z_dev(n):
        return (y * 8 + lax.rem(z + n, 4) * 2 + core, x)

    cs = []
    for n in range(1, 4):
        c = remote(mass.at[lax.rem(y + n, 4)], m1.at[y], s1.at[n], r1.at[n], y_dev(n))
        c.start()
        cs.append(c)
    m1[y] = mass[y]
    for c in cs:
        c.wait()
    total = (m1[0] + m1[1]) + (m1[2] + m1[3])
    for i in range(8):
        m2s[i] = jnp.broadcast_to(total[i : i + 1], (8, 128))
    cs = []
    for n in range(1, 8):
        to = lax.rem(row + n, 8)
        c = remote(m2s.at[to], m2.at[row], s2.at[n], r2.at[n], (y * 8 + to, x))
        c.start()
        cs.append(c)
    m2[row] = m2s[row]
    for c in cs:
        c.wait()
    label = jnp.concatenate([jnp.log1p(m2[i, 0:1]) for i in range(8)], axis=0)
    resid = ((pred[...] - label) * live[...] * norm).astype(BF16).astype(F32)
    wide = jnp.concatenate([resid, jnp.zeros((120, 128), F32)], axis=0)
    back = jnp.dot(wide.T.astype(BF16), wo[...], preferred_element_type=F32)
    delta = (back * sp[...]).astype(BF16)
    dl[j] = delta
    step = 1 - 2 * core
    ahead = lax.rem(x + step + 4, 4)
    behind = lax.rem(x - step + 4, 4)
    far = lax.rem(x + 2, 4)
    other = (seq + step, x)

    def give(slot, n, dev):
        return remote(dl.at[slot], dl.at[slot], s3.at[n], r3.at[n], dev)

    base = core * 4
    g_a = give(j, 0, (seq, ahead))
    g_b = give(j, 1, (seq, behind))
    h_0 = give(j, 3, other)
    g_a.start()
    g_b.start()
    h_0.start()
    termT = jnp.dot(wide.astype(BF16), act[...], preferred_element_type=F32)[0:8]
    bias = jnp.sum(delta.astype(F32), axis=0, keepdims=True)
    for i in range(4):
        pk[i] = termT[:, i * 256 : (i + 1) * 256]
    pk[4, :, 0:128] = resid
    for i in range(8):
        pk[4, i : i + 1, 128:256] = bias[:, i * 128 : (i + 1) * 128]
    for i in range(5, 8):
        pk[i] = jnp.zeros((8, 256), F32)
    cs = []
    for n in range(1, 8):
        c = remote(
            pk.at[lax.rem(j + n, 8)], p1.at[j], s4.at[n], r4.at[n], group_peer(seq, x, core, n)
        )
        c.start()
        cs.append(c)
    p1[j] = pk[j]
    g_a.wait_recv()
    g_c = give(base + behind, 2, (seq, ahead))
    g_c.start()
    h_1 = give(base + behind, 4, other)
    h_1.start()
    g_b.wait_recv()
    h_2 = give(base + ahead, 5, other)
    h_2.start()
    for c in cs:
        c.wait()
    t = p1[0]
    for i in range(1, 8):
        t = t + p1[i]
    p2[y] = t
    cs = []
    for n in range(1, 4):
        c = remote(p2.at[y], p2.at[y], s5.at[n], r5.at[n], y_dev(n))
        c.start()
        cs.append(c)
    g_c.wait_recv()
    h_3 = give(base + far, 6, other)
    h_3.start()
    for c in cs:
        c.wait()
    p3[z] = (p2[0] + p2[1]) + (p2[2] + p2[3])
    zs = []
    for n in range(1, 4):
        c = remote(p3.at[z], p3.at[z], s6.at[n], r6.at[n], z_dev(n))
        c.start()
        zs.append(c)
    for c in (h_0, h_1, h_2, h_3):
        c.wait()
    g_a.wait_send()
    g_b.wait_send()
    g_c.wait_send()

    d_all = dl[...].reshape(1024, 1024)
    f_all = ft[...].reshape(768, 1024)
    a_all = jnp.dot(f_all, d_all[:, 0:512], preferred_element_type=F32).reshape(4, 4, 48, 512)
    ga[...] = a_all.astype(BF16)
    own_a[...] = a_all
    acs = []
    for n in range(1, 4):
        c = remote(ga.at[lax.rem(y + n, 4)], ra.at[y], sa.at[n], qa.at[n], y_dev(n))
        c.start()
        acs.append(c)
    b_all = jnp.dot(f_all, d_all[:, 512:1024], preferred_element_type=F32).reshape(4, 4, 48, 512)
    gb[...] = b_all.astype(BF16)
    own_b[...] = b_all
    bcs = []
    for n in range(1, 4):
        c = remote(gb.at[:, lax.rem(z + n, 4)], rb.at[z], sb.at[n], qb.at[n], z_dev(n))
        c.start()
        bcs.append(c)
    for c in zs:
        c.wait()
    small[j] = (p3[0] + p3[1]) + (p3[2] + p3[3])
    fin = []
    for n in range(1, 8):
        c = remote(
            small.at[j], small.at[j], s7.at[n], r7.at[n], group_peer(seq, x, core, n)
        )
        c.start()
        fin.append(c)
    for c in acs:
        c.wait()
    sum_a = own_a[y]
    for n in range(1, 4):
        sum_a = sum_a + ra[lax.rem(y + n, 4)].astype(F32)
    pa[...] = sum_a
    acs = []
    for n in range(1, 4):
        c = remote(pa.at[lax.rem(z + n, 4)], ta.at[z], s8.at[n], r8.at[n], z_dev(n))
        c.start()
        acs.append(c)
    for c in bcs:
        c.wait()
    sum_b = own_b[:, z]
    for n in range(1, 4):
        sum_b = sum_b + rb[lax.rem(z + n, 4)].astype(F32)
    pb[...] = sum_b
    bcs = []
    for n in range(1, 4):
        c = remote(pb.at[lax.rem(y + n, 4)], tb.at[y], s9.at[n], r9.at[n], y_dev(n))
        c.start()
        bcs.append(c)
    for c in acs:
        c.wait()
    t = pa[z]
    for n in range(1, 4):
        t = t + ta[lax.rem(z + n, 4)]
    out[:, 0:512] = t
    for c in bcs:
        c.wait()
    t = pb[y]
    for n in range(1, 4):
        t = t + tb[lax.rem(y + n, 4)]
    out[:, 512:1024] = t
    for c in fin:
        c.wait()


def reduce_all(norm, mass, sp, act, pred, live, wo, ft):
    dma = pltpu.SemaphoreType.DMA
    vmem = pl.BlockSpec(memory_space=VM)
    return pl.pallas_call(
        functools.partial(reduce_kernel, norm),
        name="reduce_all",
        out_shape=(
            jax.ShapeDtypeStruct((48, 1024), F32),
            jax.ShapeDtypeStruct((8, 8, 256), F32),
        ),
        in_specs=[vmem] * 7,
        out_specs=(vmem,) * 2,
        scratch_shapes=[
            VM((4, 8, 128), F32), VM((8, 8, 128), F32), VM((8, 8, 128), F32),
            VM((8, 128, 1024), BF16),
            VM((4, 4, 48, 512), BF16), VM((4, 4, 48, 512), BF16),
            VM((4, 4, 48, 512), F32), VM((4, 4, 48, 512), F32),
            VM((4, 4, 48, 512), BF16), VM((4, 4, 48, 512), BF16),
            VM((4, 48, 512), F32), VM((4, 48, 512), F32),
            VM((4, 48, 512), F32), VM((4, 48, 512), F32),
            VM((8, 8, 256), F32), VM((8, 8, 256), F32), VM((4, 8, 256), F32), VM((4, 8, 256), F32),
        ]
        + [dma((4,)), dma((4,)), dma((8,)), dma((8,)), dma((8,)), dma((8,)), dma((8,)), dma((8,))]
        + [dma((4,)), dma((4,)), dma((4,)), dma((4,)), dma((4,)), dma((4,)), dma((4,)), dma((4,))]
        + [dma((8,)), dma((8,)), dma((4,)), dma((4,)), dma((4,)), dma((4,))],
        compiler_params=pltpu.CompilerParams(
            collective_id=1, has_side_effects=True, vmem_limit_bytes=56 * 2**20
        ),
    )(mass, sp, act, pred, live, wo, ft)


def on_device(queries, keys, values, lengths, block_pos, w_in, b_in, output_weight, output_bias):
    seq = lax.axis_index("seq")
    order = block_pos[0]
    limit = lengths[0]
    wo = jnp.pad(output_weight.T, ((0, 120), (0, 0)))
    bo = jnp.broadcast_to(output_bias[:, None], (8, 128))
    meta = jnp.concatenate(
        [order, limit[None], (seq // 8 * 8)[None].astype(jnp.int32), jnp.zeros((94,), jnp.int32)]
    )
    offsets = jnp.arange(128, dtype=jnp.int32)
    mine = lax.dynamic_index_in_dim(order, seq, 0, keepdims=False) * 128 + offsets
    live = (mine < limit).astype(F32)[None, :]
    norm = 1.0 / math.sqrt(4 * 4096)
    qg, kg, ft, sp, act, pred = spread(
        queries[0], keys[0], values[0], w_in, b_in[None, :], wo, bo
    )
    mass = column_mass(meta, qg, kg)
    grad, small = reduce_all(norm, mass.reshape(4, 8, 128), sp, act, pred, live, wo, ft)
    term = jnp.concatenate([small[i] for i in range(4)], axis=1).T
    bias = small[4, :, 128:256].reshape(1024)
    last = jnp.sum(small[4, :, 0:128], axis=1)
    return (grad, bias, term, last)


def solution(mesh):
    return jax.shard_map(
        on_device,
        mesh=mesh,
        in_specs=(
            P("batch", "seq", None),
            P("batch", "seq", None),
            P("batch", "seq", None),
            P("batch"),
            P("batch", None),
            P(),
            P(),
            P(),
            P(),
        ),
        out_specs=(P(("seq", "batch"), None), P(), P(), P()),
        check_vma=False,
    )
```

time: 520 us -> 117 us (0.23)
  waiting for transfers between devices: 229 us -> 0 us
  matrix products: 156 us -> 0 us
  Pallas kernels: 0 us -> 100 us
  blocking collectives: 66.5 us -> 0 us
  other arithmetic: 24.9 us -> 5.66 us
  between operations: 14.8 us -> 1.39 us
  local copies, waits for them, and re-layouts: 19.4 us -> 8.25 us
  starting transfers between devices: 5.78 us -> 0 us
    reduce_scatter x1 -> x0, waiting for transfers between devices: 177 us -> none  [on_device(): lax.psum_scatter(lax.dot_general(features, delta, (((0,), (0,)), ((), ())...]
    pallas_call x0 -> x3, Pallas kernels: none -> 100 us  [the longest x1 60.4 us: reduce_all(): pl.pallas_call(functools.partial(reduce_kernel, norm), name='reduce_all',...]
    div x8 -> x0, matrix products: 68.8 us -> none  [group_mass(): share = weights / denom * query_live[None, :, None]]
    sub x8 -> x0, matrix products: 67 us -> none  [group_mass(): weights = jnp.where(allowed[None], jnp.exp(masked - top), 0.0)]
    psum x1 -> x0, blocking collectives: 66.5 us -> none  [in_one(): so_far = lax.psum(jnp.concatenate([a.ravel() for a in arrays]), axis)]
    all_gather x1 -> x0, waiting for transfers between devices: 51.6 us -> none  [on_device(): every_key = lax.all_gather(k_rows, 'seq', axis=0, tiled=True)]
    dot_general x5 -> x0, matrix products: 20.6 us -> none  [the longest x1 13.2 us: on_device(): lax.dot_general(features, delta, (((0,), (0,)), ((), ())), preferred_elem...]
    dynamic_update_slice x8 -> x0, local copies, waits for them, and re-layouts: 12.9 us -> none  [group_mass(): return lax.dynamic_update_index_in_dim(sums, column, index, 0)]
  transfers between devices with their start and end apart: 3 -> 0, of which waited for: 3 -> 0; matrix products, arithmetic and copies ran while one was open for 3% -> 0% of each run, Pallas kernels for 0% -> 0%
where the time goes in v1:
time: 117 us; the launch traced here: 116 us
  Pallas kernels  100 us (85%)
  local copies, waits for them, and re-layouts  8.25 us (7%)
  other arithmetic  5.66 us (5%)
  between operations  1.39 us (1%)
    pallas_call x1, Pallas kernels, reduce_all(): pl.pallas_call(functools.partial(reduce_kernel, norm), name='reduce_all',...  60.4 us
    pallas_call x1, Pallas kernels, spread(): pl.pallas_call(spread_kernel, name='spread', out_shape=(jax.ShapeDtypeStr...  29.2 us
    pallas_call x1, Pallas kernels, column_mass(): pl.pallas_call(mass_kernel, name='column_mass', out_shape=jax.ShapeDtypeS...  10.8 us
    unnamed x19, local copies, waits for them, and re-layouts  6.04 us

profile of v1, /device:TPU:1, one launch (start us, length us, event | category | flops | bytes accessed | tf_op | source)
XLA Modules:
  0.0 115.7 jit_solution(9002295799497276130)
XLA Ops:
  1.3 1.2 %fusion = s32[1,1]{1,0:T(1,128)} fusion(s32[1,32]{1,0:T(1,128)} %param.13, s32[]{:T(128)S(6)} %select_n.10), kind=kLoop, calls=%fused_computation.10 | loop fusion | flops 1 | bytes 12 | tf_op jit(solution)/shard_map/mul | solution.py:502
  2.5 1.2 %compare_convert_fusion.live = f32[1,128]{1,0:T(1,128)} fusion(s32[]{:T(128)} %bitcast.22, s32[]{:T(128)} %bitcast.8), kind=kLoop, calls=%fused_computation.7 | loop fusion | flops 384 | bytes 520 | tf_op jit(solution)/shard_map/convert_element_type | solution.py:503
  3.7 0.7 pad_add_fusion.meta
  4.4 0.7 broadcast_in_dim.19.bo
  5.2 0.7 pad.4.wo
  5.9 0.0 copy-start.1
  5.9 1.2 %copy-done.1 = bf16[1,128,4096]{2,1,0:T(8,128)(2,1)S(1)} copy-done((bf16[1,128,4096]{2,1,0:T(8,128)(2,1)S(1)}, bf16[1,128,4096]{2,1,0:T(8,128)(2,1)}, u32[]{:S(2)}) %copy-start.1) | copy-done | bytes 1048600
  7.1 0.0 copy-start.3
  7.1 0.9 copy-done.3
  8.1 0.0 copy-start.4
  8.1 0.9 copy-done.4
  9.0 0.0 copy-start.7
  9.0 0.7 copy-done.7
  9.7 0.0 copy-start
  9.7 29.2 %spread.1 = (bf16[8,128,512]{2,1,0:T(8,128)(2,1)S(1)}, bf16[32,128,128]{2,1,0:T(8,128)(2,1)S(1)}, bf16[16,48,1024]{2,1,0:T(8,128)(2,1)}, f32[128,1024]{1,0:T(8,1...) custom-call(bf16[128,4096]{1,0:T(8,128)(2,1)S(1)} %bitcast.23, bf16[128,1024]{1,0:T(8,128)(2,1)S(1)} %bitcast.24, ...), custom_call_target="tpu_custom_call" | custom-call | tf_op jit(solution)/shard_map/spread/pallas_call | solution.py:171
  38.9 0.0 copy-start.2
  38.9 0.0 copy-start.5
  38.9 0.0 copy-start.8
  38.9 10.8 %column_mass.1 = f32[32,128]{1,0:T(8,128)S(1)} custom-call(s32[128]{0:T(128)S(1)} %pad_add_fusion.meta, bf16[8,128,512]{2,1,0:T(8,128)(2,1)S(1)} %get-tuple-element.12.qg, bf16[32,128,128]{2,1,0:T(8,128)(2,1)S(1)} %get-tuple-element.13.kg), custom_call_target="tpu_custom_call" | custom-call | tf_op jit(solution)/shard_map/column_mass/pallas_call | solution.py:272
  49.7 0.0 copy-done.2
  49.8 0.0 copy-done.5
  49.8 0.0 copy-done.8
  49.8 0.0 copy-start.6
  49.8 0.6 copy-done.6
  50.4 0.0 copy-done
  50.4 60.4 %reduce_all.1 = (f32[48,1024]{1,0:T(8,128)}, f32[8,8,256]{2,1,0:T(8,128)}) custom-call(f32[4,8,128]{2,1,0:T(8,128)} %bitcast.26, f32[128,1024]{1,0:T(8,128)} %copy-done.2, bf16[128,1024]{1,0:T(8,128)(2,1)} %copy-done.5, f32[8,128]{1,0:T(8,128)} %copy-done.8, f32[1,128]{1,0:T(1,128)} %compare_convert_fusion.live, bf16[128,1024]{1,0:T(8,128)(2,1)} %copy-done, ...), custom_call_target="tpu_custom_call" | custom-call | tf_op jit(solution)/shard_map/reduce_all/pallas_call | solution.py:464
  110.8 1.9 %slice_reduce_fusion = (f32[8]{0:T(128)}, f32[1024]{0:T(1024)}) fusion(f32[8,8,256]{2,1,0:T(8,128)} %get-tuple-element.19), kind=kLoop, calls=%fused_computation.5 | loop fusion | flops 1016 | bytes 12320 | tf_op jit(solution)/shard_map/reduce_sum | solution.py:512
  112.7 0.7 slice_bitcast_fusion.3
  113.5 0.6 maximum_bitcast_fusion
  114.1 1.6 %copy.15 = f32[48,1024]{1,0:T(8,128)} copy(f32[48,1024]{1,0:T(8,128)} %get-tuple-element.30) | data formatting | bytes 393216
  (1 shorter events, 0.0 us)
Async XLA Ops:
  5.9 1.2 %copy-start.1 = (bf16[1,128,4096]{2,1,0:T(8,128)(2,1)S(1)}, bf16[1,128,4096]{2,1,0:T(8,128)(2,1)}, u32[]{:S(2)}) copy-start(bf16[1,128,4096]{2,1,0:T(8,128)(2,1)} %param.9) | copy-start | bytes 3145732
  7.1 0.9 copy-start.3
  8.1 0.9 copy-start.4
  9.0 0.7 copy-start.7
  9.7 40.7 %copy-start = (bf16[128,1024]{1,0:T(8,128)(2,1)}, bf16[128,1024]{1,0:T(8,128)(2,1)S(1)}, u32[]{:S(2)}) copy-start(bf16[128,1024]{1,0:T(8,128)(2,1)S(1)} %pad.4.wo) | copy-start | bytes 786436
  38.9 10.8 %copy-start.2 = (f32[128,1024]{1,0:T(8,128)}, f32[128,1024]{1,0:T(8,128)S(1)}, u32[]{:S(2)}) copy-start(f32[128,1024]{1,0:T(8,128)S(1)} %get-tuple-element.14.sp) | copy-start | bytes 1572868
  38.9 10.8 %copy-start.5 = (bf16[128,1024]{1,0:T(8,128)(2,1)}, bf16[128,1024]{1,0:T(8,128)(2,1)S(1)}, u32[]{:S(2)}) copy-start(bf16[128,1024]{1,0:T(8,128)(2,1)S(1)} %get-tuple-element.15.act) | copy-start | bytes 786436
  38.9 10.8 %copy-start.8 = (f32[8,128]{1,0:T(8,128)}, f32[8,128]{1,0:T(8,128)S(1)}, u32[]{:S(2)}) copy-start(f32[8,128]{1,0:T(8,128)S(1)} %get-tuple-element.16.pred) | copy-start | bytes 12292
  49.8 0.6 copy-start.6

commit v2 on v1

v2 whole, which is shorter than its diff:
```python
import functools
import math

import jax
import jax.numpy as jnp
from jax import lax
from jax.experimental import pallas as pl
from jax.experimental.pallas import tpu as pltpu
from jax.sharding import PartitionSpec as P

MESH = pl.DeviceIdType.MESH
F32 = jnp.float32
BF16 = jnp.bfloat16
VM = pltpu.VMEM
CK = 512
WK = 512
KW = 2
FP = 4


def place():
    seq = lax.axis_index("seq")
    x = lax.axis_index("batch")
    y = seq // 8
    row = lax.rem(seq, 8)
    core = lax.rem(seq, 2)
    return seq, x, y, row, core


def greet(seq, x, y, row, core):
    bar = pltpu.get_barrier_semaphore()
    n = 0
    for k in range(1, 8):
        pl.semaphore_signal(
            bar, inc=1, device_id=(y * 8 + lax.rem(row + k, 8), x), device_id_type=MESH
        )
        n += 1
    for k in range(1, 4):
        pl.semaphore_signal(
            bar, inc=1, device_id=(lax.rem(y + k, 4) * 8 + row, x), device_id_type=MESH
        )
        n += 1
    for k in range(1, 8):
        pl.semaphore_signal(bar, inc=1, device_id=group_peer(seq, x, core, k), device_id_type=MESH)
        n += 1
    pl.semaphore_wait(bar, n)


def group_rank(x, core):
    return core * 4 + x


def group_peer(seq, x, core, k):
    j = lax.rem(group_rank(x, core) + k, 8)
    return (seq - core + j // 4, lax.rem(j, 4))


def remote(src, dst, ss, rs, dev):
    return pltpu.make_async_remote_copy(
        src_ref=src, dst_ref=dst, send_sem=ss, recv_sem=rs, device_id=dev, device_id_type=MESH
    )


def spread_kernel(
    q_hbm, k_hbm, v_hbm, w_hbm, b_in, wo, bo, qg, kg, ft_all, sp, act, pred, wot,
    q, k, v, ft, wbuf, pre, wsem, isem, ks, kr, qs, qr, fs, fr, ys, yr, ls,
):
    seq, x, y, row, core = place()
    j = group_rank(x, core)
    chunks = w_hbm.shape[0] // WK
    ins = [
        pltpu.make_async_copy(k_hbm, k, isem.at[0]),
        pltpu.make_async_copy(q_hbm, q, isem.at[1]),
        pltpu.make_async_copy(v_hbm, v, isem.at[2]),
    ]
    for c in ins:
        c.start()

    def fetch(i):
        return pltpu.make_async_copy(
            w_hbm.at[pl.ds(i * WK, WK)], wbuf.at[i % 3], wsem.at[i % 3]
        )

    fetch(0).start()
    fetch(1).start()
    greet(seq, x, y, row, core)
    kc, qc, fc, yc = [], [], [], []
    ins[0].wait()
    for n in range(1, 8):
        to = lax.rem(row + n, 8)
        c = remote(
            k.at[:, pl.ds(pl.multiple_of(to * 128, 128), 128)], kg.at[seq],
            ks.at[n], kr.at[n], (y * 8 + to, x),
        )
        c.start()
        kc.append(c)
    own_k = pltpu.make_async_copy(
        k.at[:, pl.ds(pl.multiple_of(row * 128, 128), 128)], kg.at[seq], ls.at[0]
    )
    own_k.start()
    ins[1].wait()
    for n in range(1, 8):
        to = lax.rem(row + n, 8)
        c = remote(
            q.at[:, pl.ds(pl.multiple_of(to * 512, 512), 512)], qg.at[row],
            qs.at[n], qr.at[n], (y * 8 + to, x),
        )
        c.start()
        qc.append(c)
    own_q = pltpu.make_async_copy(
        q.at[:, pl.ds(pl.multiple_of(row * 512, 512), 512)], qg.at[row], ls.at[1]
    )
    own_q.start()
    ins[2].wait()
    lanes = pl.ds(pl.multiple_of(j * 128, 128), 128)
    own_f = []
    for part in range(FP):
        span = 16 // FP
        for i in range(part * span, part * span + span):
            pieces = []
            for t in range(3):
                col = i * 384 + t * 128
                if col < 4096:
                    pieces.append(q[:, col : col + 128])
                elif col < 5120:
                    pieces.append(k[:, col - 4096 : col - 3968])
                else:
                    pieces.append(v[:, col - 5120 : col - 4992])
            block = jnp.concatenate(pieces, axis=1).astype(F32).T.astype(BF16)
            for t in range(8):
                ft[i, t] = block[t * 48 : (t + 1) * 48]
        some = pl.ds(part * span, span)
        for n in range(1, 8):
            to = lax.rem(j + n, 8)
            c = remote(
                ft.at[some, to], ft_all.at[some, :, lanes],
                fs.at[part * 8 + n], fr.at[part * 8 + n], group_peer(seq, x, core, n),
            )
            c.start()
            fc.append(c)
        c = pltpu.make_async_copy(ft.at[some, j], ft_all.at[some, :, lanes], ls.at[2 + part])
        c.start()
        own_f.append(c)

    def multiply(i):
        if i + 2 < chunks:
            fetch(i + 2).start()
        fetch(i).wait()
        lo = i * WK
        if lo < 4096:
            a = q[:, lo : lo + WK]
        elif lo < 5120:
            a = k[:, lo - 4096 : lo - 4096 + WK]
        else:
            a = v[:, lo - 5120 : lo - 5120 + WK]
        part = jnp.dot(a, wbuf[i % 3], preferred_element_type=F32)
        pre[...] = part if i == 0 else pre[...] + part

    def pass_on(n):
        block = kg.at[y * 8 + lax.rem(row + 8 - n, 8)]
        for m in range(1, 4):
            c = remote(
                block, block, ys.at[n * 4 + m], yr.at[n * 4 + m],
                (lax.rem(y + m, 4) * 8 + row, x),
            )
            c.start()
            yc.append(c)

    own_k.wait()
    pass_on(0)
    for i in range(KW):
        multiply(i)
    for n in range(1, 8):
        kc[n - 1].wait_recv()
        pass_on(n)
    for i in range(KW, chunks):
        multiply(i)
    z = pre[...] + b_in[...]
    sig = jax.nn.sigmoid(z)
    a = (z * sig).astype(BF16)
    act[...] = a
    sp[...] = sig * (1.0 + z * (1.0 - sig))
    turned = jnp.concatenate([wo[...], jnp.zeros((120, 1024), BF16)], axis=0)
    wot[...] = turned
    p8 = lax.dot_general(turned, a, (((1,), (1,)), ((), ())), preferred_element_type=F32)
    for g in range(8):
        pred[g : g + 1] = p8[g : g + 1] + bo[g]
    for c in qc + fc + yc:
        c.wait()
    for c in kc:
        c.wait_send()
    own_q.wait()
    for c in own_f:
        c.wait()


def spread(q, k, v, w, b_in, wo, bo):
    dma = pltpu.SemaphoreType.DMA
    vmem = pl.BlockSpec(memory_space=VM)
    hbm = pl.BlockSpec(memory_space=pltpu.HBM)
    return pl.pallas_call(
        spread_kernel,
        name="spread",
        out_shape=(
            jax.ShapeDtypeStruct((8, 128, 512), BF16),
            jax.ShapeDtypeStruct((32, 128, 128), BF16),
            jax.ShapeDtypeStruct((16, 48, 1024), BF16),
            jax.ShapeDtypeStruct((128, 1024), F32),
            jax.ShapeDtypeStruct((128, 1024), BF16),
            jax.ShapeDtypeStruct((8, 128), F32),
            jax.ShapeDtypeStruct((128, 1024), BF16),
        ),
        in_specs=[hbm, hbm, hbm, hbm, vmem, vmem, pl.BlockSpec(memory_space=pltpu.SMEM)],
        out_specs=(vmem,) * 7,
        scratch_shapes=[
            VM((128, 4096), BF16),
            VM((128, 1024), BF16),
            VM((128, 1024), BF16),
            VM((16, 8, 48, 128), BF16),
            VM((3, WK, 1024), BF16),
            VM((128, 1024), F32),
            dma((3,)), dma((3,)),
            dma((8,)), dma((8,)), dma((8,)), dma((8,)),
            dma((8 * FP,)), dma((8 * FP,)), dma((32,)), dma((32,)),
            dma((2 + FP,)),
        ],
        compiler_params=pltpu.CompilerParams(
            collective_id=0, has_side_effects=True, vmem_limit_bytes=40 * 2**20
        ),
    )(q, k, v, w, b_in, wo, bo)


def mass_kernel(meta, length, qg, kg, out, live, kpos, s_ref, acc):
    seq, _, y, _, _ = place()
    limit = length[0]
    first = y * 8
    here = lax.broadcasted_iota(jnp.int32, (1, 128), 1) + meta[seq] * 128
    live[...] = (here < limit).astype(F32)
    factor = math.log2(math.e) / math.sqrt(128)

    def order(r, _):
        kpos[pl.ds(pl.multiple_of(meta[r] * 128, 128), 128)] = kg[r]
        return 0

    lax.fori_loop(0, 32, order, 0)
    acc[...] = jnp.zeros_like(acc)
    lane = lax.rem(lax.broadcasted_iota(jnp.int32, (1, 512), 1), 128)
    sub = lax.broadcasted_iota(jnp.int32, (CK, 512), 0)

    def fold(a, op):
        return op(a.reshape(CK // 8, 8, 512), axis=0)

    def block(i, _):
        pos = meta[first + i]

        @pl.when(pos * 128 < limit)
        def _():
            last = pos * 128 // CK
            q4 = jnp.concatenate([qg[i, :, h * 128 : (h + 1) * 128] for h in range(4)], axis=0)

            def scores(c):
                rows = pl.ds(pl.multiple_of(c * CK, CK), CK)
                return rows, lax.dot_general(
                    kpos[rows], q4, (((1,), (1,)), ((), ())), preferred_element_type=F32
                )

            def first_pass(c, top):
                rows, s = scores(c)
                s_ref[rows] = s
                return jnp.maximum(top, fold(s, jnp.max))

            top = lax.fori_loop(0, last, first_pass, jnp.full((8, 512), -1e30, F32))
            rows, s = scores(last)
            s = jnp.where(sub + last * CK <= lane + pos * 128, s, -1e30)
            s_ref[rows] = s
            top = jnp.max(jnp.maximum(top, fold(s, jnp.max)), axis=0, keepdims=True)

            def second_pass(c, total):
                rows = pl.ds(pl.multiple_of(c * CK, CK), CK)
                e = jnp.exp2((s_ref[rows] - top) * factor)
                s_ref[rows] = e
                return total + fold(e, jnp.sum)

            total = lax.fori_loop(0, last + 1, second_pass, jnp.zeros((8, 512), F32))
            total = jnp.sum(total, axis=0, keepdims=True)
            share = jnp.where(lane + pos * 128 < limit, 1.0 / total, 0.0)

            def third_pass(c, _):
                rows = pl.ds(pl.multiple_of(c * CK, CK), CK)
                e = s_ref[rows] * share
                acc[rows] += (e[:, 0:128] + e[:, 128:256]) + (e[:, 256:384] + e[:, 384:512])
                return 0

            lax.fori_loop(0, last + 1, third_pass, 0)

        return 0

    lax.fori_loop(0, 8, block, 0)

    def give(r, _):
        rows = acc[pl.ds(pl.multiple_of(meta[r] * 128, 128), 128)]
        out[pl.ds(r, 1)] = jnp.sum(rows.T, axis=0, keepdims=True)
        return 0

    lax.fori_loop(0, 32, give, 0)


def column_mass(order, length, qg, kg):
    smem = pl.BlockSpec(memory_space=pltpu.SMEM)
    vmem = pl.BlockSpec(memory_space=VM)
    return pl.pallas_call(
        mass_kernel,
        name="column_mass",
        out_shape=(jax.ShapeDtypeStruct((32, 128), F32), jax.ShapeDtypeStruct((1, 128), F32)),
        in_specs=[smem, smem, vmem, vmem],
        out_specs=(vmem, vmem),
        scratch_shapes=[VM((4096, 128), BF16), VM((4096, 512), F32), VM((4096, 128), F32)],
        compiler_params=pltpu.CompilerParams(vmem_limit_bytes=40 * 2**20),
    )(order, length, qg, kg)


def reduce_kernel(
    norm, mass, sp, act, pred, live, wo, ft, out, small,
    m1, m2s, m2, dl, gs, res, rs, ps, ts, pk, p1, p2, p3,
    s1, r1, s2, r2, s3, r3, s4, r4, s5, r5, s6, r6, s7, r7, s8, r8, s9, r9,
):
    seq, x, y, row, core = place()
    z = row // 2
    j = group_rank(x, core)
    greet(seq, x, y, row, core)

    def y_dev(n):
        return (lax.rem(y + n, 4) * 8 + row, x)

    def z_dev(n):
        return (y * 8 + lax.rem(z + n, 4) * 2 + core, x)

    cs = []
    for n in range(1, 4):
        c = remote(mass.at[lax.rem(y + n, 4)], m1.at[y], s1.at[n], r1.at[n], y_dev(n))
        c.start()
        cs.append(c)
    m1[y] = mass[y]
    for c in cs:
        c.wait()
    total = (m1[0] + m1[1]) + (m1[2] + m1[3])
    for i in range(8):
        m2s[i] = jnp.broadcast_to(total[i : i + 1], (8, 128))
    cs = []
    for n in range(1, 8):
        to = lax.rem(row + n, 8)
        c = remote(m2s.at[to], m2.at[row], s2.at[n], r2.at[n], (y * 8 + to, x))
        c.start()
        cs.append(c)
    m2[row] = m2s[row]
    for c in cs:
        c.wait()
    label = jnp.concatenate([jnp.log1p(m2[i, 0:1]) for i in range(8)], axis=0)
    resid = ((pred[...] - label) * live[...] * norm).astype(BF16).astype(F32)
    wide = jnp.concatenate([resid, jnp.zeros((120, 128), F32)], axis=0)
    back = jnp.dot(wide.T.astype(BF16), wo[...], preferred_element_type=F32)
    delta = (back * sp[...]).astype(BF16)
    other = (seq + 1 - 2 * core, x)
    base = core * 4
    for p in range(4):
        dl[p, j] = delta[:, p * 256 : (p + 1) * 256]

    def give(p, slot, n, dev):
        return remote(dl.at[p, slot], dl.at[p, slot], s3.at[p * 8 + n], r3.at[p * 8 + n], dev)

    direct = [[give(p, j, n, (seq, lax.rem(x + n, 4))) for n in (2, 1, 3)] for p in range(4)]
    passed = [
        [give(p, base + lax.rem(x + 4 - n, 4), 4 + n, other) for n in (0, 2, 1, 3)]
        for p in range(4)
    ]
    for p in range(4):
        for c in direct[p]:
            c.start()
        passed[p][0].start()
    term = jnp.dot(wide.astype(BF16), act[...], preferred_element_type=F32)[0:8]
    bias = jnp.sum(delta.astype(F32), axis=0, keepdims=True)
    for i in range(4):
        pk[i] = term[:, i * 256 : (i + 1) * 256]
    pk[4, :, 0:128] = resid
    for i in range(8):
        pk[4, i : i + 1, 128:256] = bias[:, i * 128 : (i + 1) * 128]
    for i in range(5, 8):
        pk[i] = jnp.zeros((8, 256), F32)
    xs = []
    for n in range(1, 8):
        c = remote(
            pk.at[lax.rem(j + n, 8)], p1.at[j], s4.at[n], r4.at[n], group_peer(seq, x, core, n)
        )
        c.start()
        xs.append(c)
    p1[j] = pk[j]

    first, second = [], []

    def fold(h):
        for c in first[h]:
            c.wait()
        if h % 2 == 0:
            t = res[h, y]
            for n in range(1, 4):
                t = t + rs[h, lax.rem(y + n, 4)].astype(F32)
        else:
            t = res[h, :, z]
            for n in range(1, 4):
                t = t + rs[h, lax.rem(z + n, 4)].astype(F32)
        ps[h] = t
        cs = []
        for n in range(1, 4):
            if h % 2 == 0:
                c = remote(
                    ps.at[h, lax.rem(z + n, 4)], ts.at[h, z],
                    s9.at[h * 4 + n], r9.at[h * 4 + n], z_dev(n),
                )
            else:
                c = remote(
                    ps.at[h, lax.rem(y + n, 4)], ts.at[h, y],
                    s9.at[h * 4 + n], r9.at[h * 4 + n], y_dev(n),
                )
            c.start()
            cs.append(c)
        second.append(cs)

    f_all = ft[...].reshape(768, 1024)
    for p in range(4):
        for c, d in zip(direct[p], passed[p][1:]):
            c.wait_recv()
            d.start()
        for c in passed[p]:
            c.wait_recv()
        g = jnp.dot(f_all, dl[p].reshape(1024, 256), preferred_element_type=F32)
        for h in (2 * p, 2 * p + 1):
            half = g[:, (h % 2) * 128 : (h % 2) * 128 + 128].reshape(4, 4, 48, 128)
            gs[h] = half.astype(BF16)
            res[h] = half
            cs = []
            for n in range(1, 4):
                if h % 2 == 0:
                    c = remote(
                        gs.at[h, lax.rem(y + n, 4)], rs.at[h, y],
                        s8.at[h * 4 + n], r8.at[h * 4 + n], y_dev(n),
                    )
                else:
                    c = remote(
                        gs.at[h, :, lax.rem(z + n, 4)], rs.at[h, z],
                        s8.at[h * 4 + n], r8.at[h * 4 + n], z_dev(n),
                    )
                c.start()
                cs.append(c)
            first.append(cs)
        if p >= 1:
            fold(2 * p - 2)
            fold(2 * p - 1)
        if p == 1:
            for c in xs:
                c.wait()
            t = p1[0]
            for i in range(1, 8):
                t = t + p1[i]
            p2[y] = t
            ys = []
            for n in range(1, 4):
                c = remote(p2.at[y], p2.at[y], s5.at[n], r5.at[n], y_dev(n))
                c.start()
                ys.append(c)
        if p == 3:
            for c in ys:
                c.wait()
            p3[z] = (p2[0] + p2[1]) + (p2[2] + p2[3])
            zs = []
            for n in range(1, 4):
                c = remote(p3.at[z], p3.at[z], s6.at[n], r6.at[n], z_dev(n))
                c.start()
                zs.append(c)
    for p in range(4):
        for c in direct[p] + passed[p]:
            c.wait_send()
    fold(6)
    fold(7)
    for c in zs:
        c.wait()
    small[j] = (p3[0] + p3[1]) + (p3[2] + p3[3])
    fin = []
    for n in range(1, 8):
        c = remote(small.at[j], small.at[j], s7.at[n], r7.at[n], group_peer(seq, x, core, n))
        c.start()
        fin.append(c)
    for h in range(8):
        for c in second[h]:
            c.wait()
        if h % 2 == 0:
            t = ps[h, z]
            for n in range(1, 4):
                t = t + ts[h, lax.rem(z + n, 4)]
        else:
            t = ps[h, y]
            for n in range(1, 4):
                t = t + ts[h, lax.rem(y + n, 4)]
        out[:, h * 128 : (h + 1) * 128] = t
    for c in fin:
        c.wait()


def reduce_all(norm, mass, sp, act, pred, live, wo, ft):
    dma = pltpu.SemaphoreType.DMA
    vmem = pl.BlockSpec(memory_space=VM)
    return pl.pallas_call(
        functools.partial(reduce_kernel, norm),
        name="reduce_all",
        out_shape=(
            jax.ShapeDtypeStruct((48, 1024), F32),
            jax.ShapeDtypeStruct((8, 8, 256), F32),
        ),
        in_specs=[vmem] * 7,
        out_specs=(vmem,) * 2,
        scratch_shapes=[
            VM((4, 8, 128), F32), VM((8, 8, 128), F32), VM((8, 8, 128), F32),
            VM((4, 8, 128, 256), BF16),
            VM((8, 4, 4, 48, 128), BF16),
            VM((8, 4, 4, 48, 128), F32),
            VM((8, 4, 4, 48, 128), BF16),
            VM((8, 4, 48, 128), F32),
            VM((8, 4, 48, 128), F32),
            VM((8, 8, 256), F32), VM((8, 8, 256), F32), VM((4, 8, 256), F32), VM((4, 8, 256), F32),
        ]
        + [dma((4,)), dma((4,)), dma((8,)), dma((8,)), dma((32,)), dma((32,)), dma((8,)), dma((8,))]
        + [dma((4,)), dma((4,)), dma((4,)), dma((4,)), dma((8,)), dma((8,))]
        + [dma((32,)), dma((32,)), dma((32,)), dma((32,))],
        compiler_params=pltpu.CompilerParams(
            collective_id=1, has_side_effects=True, vmem_limit_bytes=40 * 2**20
        ),
    )(mass, sp, act, pred, live, wo, ft)


def finish_kernel(g, small, grad, bias, term, last):
    grad[...] = g[...]
    bias[...] = small[4, :, 128:256]
    t = jnp.concatenate([small[i] for i in range(4)], axis=1)
    term[...] = t
    r = jnp.concatenate([small[4, :, 0:128], jnp.zeros((120, 128), F32)], axis=0).T
    last[...] = jnp.sum(r, axis=0, keepdims=True)[:, 0:8]


def finish(g, small):
    vmem = pl.BlockSpec(memory_space=VM)
    return pl.pallas_call(
        finish_kernel,
        name="finish",
        out_shape=(
            jax.ShapeDtypeStruct((48, 1024), F32),
            jax.ShapeDtypeStruct((8, 128), F32),
            jax.ShapeDtypeStruct((8, 1024), F32),
            jax.ShapeDtypeStruct((1, 8), F32),
        ),
        in_specs=[vmem] * 2,
        out_specs=(vmem,) * 4,
    )(g, small)


def on_device(queries, keys, values, lengths, block_pos, w_in, b_in, output_weight, output_bias):
    norm = 1.0 / math.sqrt(4 * 4096)
    qg, kg, ft, sp, act, pred, wot = spread(
        queries[0], keys[0], values[0], w_in, b_in[None, :], output_weight.T, output_bias
    )
    mass, live = column_mass(block_pos[0], lengths, qg, kg)
    g, small = reduce_all(norm, mass.reshape(4, 8, 128), sp, act, pred, live, wot, ft)
    grad, bias, term, last = finish(g, small)
    return (grad, bias.reshape(1024), term.T, last.reshape(8))


def solution(mesh):
    return jax.shard_map(
        on_device,
        mesh=mesh,
        in_specs=(
            P("batch", "seq", None),
            P("batch", "seq", None),
            P("batch", "seq", None),
            P("batch"),
            P("batch", None),
            P(),
            P(),
            P(),
            P(),
        ),
        out_specs=(P(("seq", "batch"), None), P(), P(), P()),
        check_vma=False,
    )
```

time: 117 us -> 104 us (0.89)
  other arithmetic: 5.66 us -> 0 us
  Pallas kernels: 100 us -> 95.6 us
  local copies, waits for them, and re-layouts: 8.25 us -> 6.47 us
    pallas_call x1, Pallas kernels: 60.4 us -> 48.1 us  [reduce_all(): pl.pallas_call(functools.partial(reduce_kernel, norm), name='reduce_all',...]
    pallas_call x1 -> x2, Pallas kernels: 10.8 us -> 19.8 us  [the longest x1 18.1 us: column_mass(): pl.pallas_call(mass_kernel, name='column_mass', out_shape=(jax.ShapeDtype...]
    reduce_sum x1 -> x0, other arithmetic: 1.91 us -> none  [on_device(): last = jnp.sum(small[4, :, 0:128], axis=1)]
    pallas_call x1, Pallas kernels: 29.2 us -> 27.7 us  [spread(): pl.pallas_call(spread_kernel, name='spread', out_shape=(jax.ShapeDtypeStr...]
    mul x1 -> x0, other arithmetic: 1.24 us -> none  [on_device(): lax.dynamic_index_in_dim(order, seq, 0, keepdims=False) * 128 + offsets]
    unnamed x19 -> x18, local copies, waits for them, and re-layouts: 6.04 us -> 6.47 us
where the time goes in v2:
time: 104 us; the launch traced here: 103 us
  Pallas kernels  95.6 us (92%)
  local copies, waits for them, and re-layouts  6.47 us (6%)
  between operations  1.36 us (1%)
    pallas_call x1, Pallas kernels, reduce_all(): pl.pallas_call(functools.partial(reduce_kernel, norm), name='reduce_all',...  48.1 us
    pallas_call x1, Pallas kernels, spread(): pl.pallas_call(spread_kernel, name='spread', out_shape=(jax.ShapeDtypeStr...  27.7 us
    pallas_call x1, Pallas kernels, column_mass(): pl.pallas_call(mass_kernel, name='column_mass', out_shape=(jax.ShapeDtype...  18.1 us
    unnamed x18, local copies, waits for them, and re-layouts  6.47 us

profile of v2, /device:TPU:1, one launch (start us, length us, event | category | flops | bytes accessed | tf_op | source)
XLA Modules:
  0.0 103.4 jit_solution(10609298531978962960)
XLA Ops:
  0.6 0.0 copy-start.8
  1.3 0.0 copy-start
  1.3 1.2 %copy-done = bf16[1,128,4096]{2,1,0:T(8,128)(2,1)S(1)} copy-done((bf16[1,128,4096]{2,1,0:T(8,128)(2,1)S(1)}, bf16[1,128,4096]{2,1,0:T(8,128)(2,1)}, u32[]{:S(2)}) %copy-start) | copy-done | bytes 1048600
  2.5 0.0 copy-start.1
  2.5 0.9 copy-done.1
  3.5 0.0 copy-start.2
  3.5 0.9 copy-done.2
  4.4 0.0 copy-start.5
  4.4 0.7 copy-done.5
  5.1 0.0 copy-start.6
  5.2 0.7 copy-done.6
  5.8 0.0 copy-start.7
  5.8 0.7 copy-done.7
  6.5 27.7 %spread.1 = (bf16[8,128,512]{2,1,0:T(8,128)(2,1)S(1)}, bf16[32,128,128]{2,1,0:T(8,128)(2,1)S(1)}, bf16[16,48,1024]{2,1,0:T(8,128)(2,1)S(1)}, f32[128,1024]{1,0:T...) custom-call(bf16[128,4096]{1,0:T(8,128)(2,1)S(1)} %bitcast.10, ...), custom_call_target="tpu_custom_call" | custom-call | tf_op jit(solution)/shard_map/spread/pallas_call | solution.py:201
  34.2 0.0 copy-done.8
  34.2 18.1 %column_mass.1 = (f32[32,128]{1,0:T(8,128)S(1)}, f32[1,128]{1,0:T(1,128)S(1)}) custom-call(s32[32]{0:T(128)S(1)} %bitcast.16, s32[1]{0:T(128)S(6)} %copy.13.length, bf16[8,128,512]{2,1,0:T(8,128)(2,1)S(1)} %get-tuple-element.19.qg, bf16[32,128,128]{2,1,0:T(8,128)(2,1)S(1)} %get-tuple-element.20.kg), custom_call_target="tpu_custom_call" | custom-call | tf_op jit(solution)/shard_map/column_mass/pallas_call | solution.py:311
  52.4 48.1 %reduce_all.1 = (f32[48,1024]{1,0:T(8,128)S(1)}, f32[8,8,256]{2,1,0:T(8,128)S(1)}) custom-call(f32[4,8,128]{2,1,0:T(8,128)S(1)} %bitcast.13, f32[128,1024]{1,0:T(8,128)S(1)} %get-tuple-element.22.sp, bf16[128,1024]{1,0:T(8,128)(2,1)S(1)} %get-tuple-element.23.act, f32[8,128]{1,0:T(8,128)S(1)} %get-tuple-element.24.pred, ...), custom_call_target="tpu_custom_call" | custom-call | tf_op jit(solution)/shard_map/reduce_all/pallas_call | solution.py:511
  100.5 0.0 copy-start.3
  100.5 0.7 copy-done.3
  101.2 0.0 copy-start.4
  101.2 0.6 copy-done.4
  101.8 1.6 %finish.1 = (f32[48,1024]{1,0:T(8,128)}, f32[8,128]{1,0:T(8,128)}, f32[8,1024]{1,0:T(8,128)}, f32[1,8]{1,0:T(1,128)}) custom-call(f32[48,1024]{1,0:T(8,128)} %copy-done.3, f32[8,8,256]{2,1,0:T(8,128)} %copy-done.4), custom_call_target="tpu_custom_call" | custom-call | tf_op jit(solution)/shard_map/finish/pallas_call | solution.py:550
Async XLA Ops:
  0.6 33.6 %copy-start.8 = (s32[1,32]{1,0:T(1,128)S(1)}, s32[1,32]{1,0:T(1,128)}, u32[]{:S(2)}) copy-start(s32[1,32]{1,0:T(1,128)} %param.13) | copy-start | bytes 388
  1.3 1.2 %copy-start = (bf16[1,128,4096]{2,1,0:T(8,128)(2,1)S(1)}, bf16[1,128,4096]{2,1,0:T(8,128)(2,1)}, u32[]{:S(2)}) copy-start(bf16[1,128,4096]{2,1,0:T(8,128)(2,1)} %param.9) | copy-start | bytes 3145732
  2.5 0.9 copy-start.1
  3.5 0.9 copy-start.2
  4.4 0.7 copy-start.5
  5.1 0.7 copy-start.6
  5.8 0.7 copy-start.7
  100.5 0.7 copy-start.3
  101.2 0.6 copy-start.4

commit v3 on v2

--- a/solution.py
+++ b/solution.py
@@ -15,6 +15,8 @@
 CK = 512
 WK = 512
 KW = 2
+PARTS = ((0, 1), (2, 3), (4, 5), (6, 7))
+EARLY = 3
 FP = 4
 
 
@@ -30,20 +32,15 @@
 def greet(seq, x, y, row, core):
     bar = pltpu.get_barrier_semaphore()
     n = 0
-    for k in range(1, 8):
-        pl.semaphore_signal(
-            bar, inc=1, device_id=(y * 8 + lax.rem(row + k, 8), x), device_id_type=MESH
-        )
-        n += 1
-    for k in range(1, 4):
-        pl.semaphore_signal(
-            bar, inc=1, device_id=(lax.rem(y + k, 4) * 8 + row, x), device_id_type=MESH
-        )
+    near = [(y * 8 + lax.rem(row + k, 8), x) for k in range(1, 8)]
+    near += [(lax.rem(y + k, 4) * 8 + row, x) for k in range(1, 4)]
+    for dev in near:
+        pl.semaphore_signal(bar, inc=1, device_id=dev, device_id_type=MESH)
         n += 1
     for k in range(1, 8):
         pl.semaphore_signal(bar, inc=1, device_id=group_peer(seq, x, core, k), device_id_type=MESH)
         n += 1
-    pl.semaphore_wait(bar, n)
+    return functools.partial(pl.semaphore_wait, bar, n)
 
 
 def group_rank(x, core):
@@ -62,15 +59,15 @@
 
 
 def spread_kernel(
-    q_hbm, k_hbm, v_hbm, w_hbm, b_in, wo, bo, qg, kg, ft_all, sp, act, pred, wot,
-    q, k, v, ft, wbuf, pre, wsem, isem, ks, kr, qs, qr, fs, fr, ys, yr, ls,
+    q_hbm, k_hbm, v_hbm, w_hbm, qg, kg, ft_all, pre,
+    q, k, v, ft, wbuf, wsem, isem, ks, kr, qs, qr, fs, fr, ys, yr, ls,
 ):
     seq, x, y, row, core = place()
     j = group_rank(x, core)
     chunks = w_hbm.shape[0] // WK
     ins = [
-        pltpu.make_async_copy(k_hbm, k, isem.at[0]),
-        pltpu.make_async_copy(q_hbm, q, isem.at[1]),
+        pltpu.make_async_copy(q_hbm, q, isem.at[0]),
+        pltpu.make_async_copy(k_hbm, k, isem.at[1]),
         pltpu.make_async_copy(v_hbm, v, isem.at[2]),
     ]
     for c in ins:
@@ -83,39 +80,14 @@
 
     fetch(0).start()
     fetch(1).start()
-    greet(seq, x, y, row, core)
-    kc, qc, fc, yc = [], [], [], []
-    ins[0].wait()
-    for n in range(1, 8):
-        to = lax.rem(row + n, 8)
-        c = remote(
-            k.at[:, pl.ds(pl.multiple_of(to * 128, 128), 128)], kg.at[seq],
-            ks.at[n], kr.at[n], (y * 8 + to, x),
-        )
-        c.start()
-        kc.append(c)
-    own_k = pltpu.make_async_copy(
-        k.at[:, pl.ds(pl.multiple_of(row * 128, 128), 128)], kg.at[seq], ls.at[0]
-    )
-    own_k.start()
-    ins[1].wait()
-    for n in range(1, 8):
-        to = lax.rem(row + n, 8)
-        c = remote(
-            q.at[:, pl.ds(pl.multiple_of(to * 512, 512), 512)], qg.at[row],
-            qs.at[n], qr.at[n], (y * 8 + to, x),
-        )
-        c.start()
-        qc.append(c)
-    own_q = pltpu.make_async_copy(
-        q.at[:, pl.ds(pl.multiple_of(row * 512, 512), 512)], qg.at[row], ls.at[1]
-    )
-    own_q.start()
-    ins[2].wait()
+    met = greet(seq, x, y, row, core)
+    for c in ins:
+        c.wait()
     lanes = pl.ds(pl.multiple_of(j * 128, 128), 128)
-    own_f = []
-    for part in range(FP):
-        span = 16 // FP
+    kc, qc, fc, yc, own_f = [], [], [], [], []
+    span = 16 // FP
+
+    def turn(part):
         for i in range(part * span, part * span + span):
             pieces = []
             for t in range(3):
@@ -129,8 +101,10 @@
             block = jnp.concatenate(pieces, axis=1).astype(F32).T.astype(BF16)
             for t in range(8):
                 ft[i, t] = block[t * 48 : (t + 1) * 48]
+
+    def send(part):
         some = pl.ds(part * span, span)
-        for n in range(1, 8):
+        for n in (2, 6, 1, 3, 5, 7, 4):
             to = lax.rem(j + n, 8)
             c = remote(
                 ft.at[some, to], ft_all.at[some, :, lanes],
@@ -141,6 +115,39 @@
         c = pltpu.make_async_copy(ft.at[some, j], ft_all.at[some, :, lanes], ls.at[2 + part])
         c.start()
         own_f.append(c)
+
+    for part in range(EARLY):
+        turn(part)
+    met()
+    for n in range(1, 8):
+        to = lax.rem(row + n, 8)
+        c = remote(
+            k.at[:, pl.ds(pl.multiple_of(to * 128, 128), 128)], kg.at[seq],
+            ks.at[n], kr.at[n], (y * 8 + to, x),
+        )
+        c.start()
+        kc.append(c)
+    own_k = pltpu.make_async_copy(
+        k.at[:, pl.ds(pl.multiple_of(row * 128, 128), 128)], kg.at[seq], ls.at[0]
+    )
+    own_k.start()
+    for part in range(EARLY):
+        send(part)
+    for n in range(1, 8):
+        to = lax.rem(row + n, 8)
+        c = remote(
+            q.at[:, pl.ds(pl.multiple_of(to * 512, 512), 512)], qg.at[row],
+            qs.at[n], qr.at[n], (y * 8 + to, x),
+        )
+        c.start()
+        qc.append(c)
+    own_q = pltpu.make_async_copy(
+        q.at[:, pl.ds(pl.multiple_of(row * 512, 512), 512)], qg.at[row], ls.at[1]
+    )
+    own_q.start()
+    for part in range(EARLY, FP):
+        turn(part)
+        send(part)
 
     def multiply(i):
         if i + 2 < chunks:
@@ -175,16 +182,6 @@
         pass_on(n)
     for i in range(KW, chunks):
         multiply(i)
-    z = pre[...] + b_in[...]
-    sig = jax.nn.sigmoid(z)
-    a = (z * sig).astype(BF16)
-    act[...] = a
-    sp[...] = sig * (1.0 + z * (1.0 - sig))
-    turned = jnp.concatenate([wo[...], jnp.zeros((120, 1024), BF16)], axis=0)
-    wot[...] = turned
-    p8 = lax.dot_general(turned, a, (((1,), (1,)), ((), ())), preferred_element_type=F32)
-    for g in range(8):
-        pred[g : g + 1] = p8[g : g + 1] + bo[g]
     for c in qc + fc + yc:
         c.wait()
     for c in kc:
@@ -194,7 +191,7 @@
         c.wait()
 
 
-def spread(q, k, v, w, b_in, wo, bo):
+def spread(q, k, v, w):
     dma = pltpu.SemaphoreType.DMA
     vmem = pl.BlockSpec(memory_space=VM)
     hbm = pl.BlockSpec(memory_space=pltpu.HBM)
@@ -206,19 +203,15 @@
             jax.ShapeDtypeStruct((32, 128, 128), BF16),
             jax.ShapeDtypeStruct((16, 48, 1024), BF16),
             jax.ShapeDtypeStruct((128, 1024), F32),
-            jax.ShapeDtypeStruct((128, 1024), BF16),
-            jax.ShapeDtypeStruct((8, 128), F32),
-            jax.ShapeDtypeStruct((128, 1024), BF16),
         ),
-        in_specs=[hbm, hbm, hbm, hbm, vmem, vmem, pl.BlockSpec(memory_space=pltpu.SMEM)],
-        out_specs=(vmem,) * 7,
+        in_specs=[hbm, hbm, hbm, hbm],
+        out_specs=(vmem,) * 4,
         scratch_shapes=[
             VM((128, 4096), BF16),
             VM((128, 1024), BF16),
             VM((128, 1024), BF16),
             VM((16, 8, 48, 128), BF16),
             VM((3, WK, 1024), BF16),
-            VM((128, 1024), F32),
             dma((3,)), dma((3,)),
             dma((8,)), dma((8,)), dma((8,)), dma((8,)),
             dma((8 * FP,)), dma((8 * FP,)), dma((32,)), dma((32,)),
@@ -227,7 +220,7 @@
         compiler_params=pltpu.CompilerParams(
             collective_id=0, has_side_effects=True, vmem_limit_bytes=40 * 2**20
         ),
-    )(q, k, v, w, b_in, wo, bo)
+    )(q, k, v, w)
 
 
 def mass_kernel(meta, length, qg, kg, out, live, kpos, s_ref, acc):
@@ -320,14 +313,14 @@
 
 
 def reduce_kernel(
-    norm, mass, sp, act, pred, live, wo, ft, out, small,
+    norm, mass, pre, b_in, wo, bo, live, ft, out, small,
     m1, m2s, m2, dl, gs, res, rs, ps, ts, pk, p1, p2, p3,
     s1, r1, s2, r2, s3, r3, s4, r4, s5, r5, s6, r6, s7, r7, s8, r8, s9, r9,
 ):
     seq, x, y, row, core = place()
     z = row // 2
     j = group_rank(x, core)
-    greet(seq, x, y, row, core)
+    greet(seq, x, y, row, core)()
 
     def y_dev(n):
         return (lax.rem(y + n, 4) * 8 + row, x)
@@ -341,6 +334,11 @@
         c.start()
         cs.append(c)
     m1[y] = mass[y]
+    lin = pre[...] + b_in[...]
+    sig = jax.nn.sigmoid(lin)
+    act = (lin * sig).astype(BF16)
+    slope = sig * (1.0 + lin * (1.0 - sig))
+    wide_o = jnp.concatenate([wo[...], jnp.zeros((120, 1024), BF16)], axis=0)
     for c in cs:
         c.wait()
     total = (m1[0] + m1[1]) + (m1[2] + m1[3])
@@ -353,31 +351,39 @@
         c.start()
         cs.append(c)
     m2[row] = m2s[row]
+    p8 = lax.dot_general(wide_o, act, (((1,), (1,)), ((), ())), preferred_element_type=F32)
+    pred = jnp.concatenate([p8[g : g + 1] + bo[g] for g in range(8)], axis=0)
     for c in cs:
         c.wait()
-    label = jnp.concatenate([jnp.log1p(m2[i, 0:1]) for i in range(8)], axis=0)
-    resid = ((pred[...] - label) * live[...] * norm).astype(BF16).astype(F32)
+    mass_t = jnp.concatenate([m2[g, 0:1] for g in range(8)], axis=0)
+    label = jnp.log1p(mass_t)
+    resid = ((pred - label) * live[...] * norm).astype(BF16).astype(F32)
     wide = jnp.concatenate([resid, jnp.zeros((120, 128), F32)], axis=0)
-    back = jnp.dot(wide.T.astype(BF16), wo[...], preferred_element_type=F32)
-    delta = (back * sp[...]).astype(BF16)
+    back = jnp.dot(wide.T.astype(BF16), wide_o, preferred_element_type=F32)
+    delta = (back * slope).astype(BF16)
     other = (seq + 1 - 2 * core, x)
     base = core * 4
-    for p in range(4):
-        dl[p, j] = delta[:, p * 256 : (p + 1) * 256]
+    for h in range(8):
+        dl[h, j] = delta[:, h * 128 : (h + 1) * 128]
+    parts = len(PARTS)
 
     def give(p, slot, n, dev):
-        return remote(dl.at[p, slot], dl.at[p, slot], s3.at[p * 8 + n], r3.at[p * 8 + n], dev)
-
-    direct = [[give(p, j, n, (seq, lax.rem(x + n, 4))) for n in (2, 1, 3)] for p in range(4)]
+        some = dl.at[pl.ds(PARTS[p][0], len(PARTS[p])), slot]
+        return remote(some, some, s3.at[p * 8 + n], r3.at[p * 8 + n], dev)
+
+    direct = [[give(p, j, n, (seq, lax.rem(x + n, 4))) for n in (2, 1, 3)] for p in range(parts)]
     passed = [
         [give(p, base + lax.rem(x + 4 - n, 4), 4 + n, other) for n in (0, 2, 1, 3)]
-        for p in range(4)
+        for p in range(parts)
     ]
-    for p in range(4):
+
+    def set_out(p):
         for c in direct[p]:
             c.start()
         passed[p][0].start()
-    term = jnp.dot(wide.astype(BF16), act[...], preferred_element_type=F32)[0:8]
+
+    set_out(0)
+    term = jnp.dot(wide.astype(BF16), act, preferred_element_type=F32)[0:8]
     bias = jnp.sum(delta.astype(F32), axis=0, keepdims=True)
     for i in range(4):
         pk[i] = term[:, i * 256 : (i + 1) * 256]
@@ -394,6 +400,8 @@
         c.start()
         xs.append(c)
     p1[j] = pk[j]
+    for p in range(1, parts):
+        set_out(p)
 
     first, second = [], []
 
@@ -426,15 +434,16 @@
         second.append(cs)
 
     f_all = ft[...].reshape(768, 1024)
-    for p in range(4):
+    for p in range(parts):
         for c, d in zip(direct[p], passed[p][1:]):
             c.wait_recv()
             d.start()
         for c in passed[p]:
             c.wait_recv()
-        g = jnp.dot(f_all, dl[p].reshape(1024, 256), preferred_element_type=F32)
-        for h in (2 * p, 2 * p + 1):
-            half = g[:, (h % 2) * 128 : (h % 2) * 128 + 128].reshape(4, 4, 48, 128)
+        d_all = jnp.concatenate([dl[h].reshape(1024, 128) for h in PARTS[p]], axis=1)
+        g = jnp.dot(f_all, d_all, preferred_element_type=F32)
+        for i, h in enumerate(PARTS[p]):
+            half = g[:, i * 128 : (i + 1) * 128].reshape(4, 4, 48, 128)
             gs[h] = half.astype(BF16)
             res[h] = half
             cs = []
@@ -452,23 +461,23 @@
                 c.start()
                 cs.append(c)
             first.append(cs)
-        if p >= 1:
-            fold(2 * p - 2)
-            fold(2 * p - 1)
-        if p == 1:
+        if p == 0:
             for c in xs:
                 c.wait()
             t = p1[0]
             for i in range(1, 8):
                 t = t + p1[i]
             p2[y] = t
-            ys = []
+            sy = []
             for n in range(1, 4):
                 c = remote(p2.at[y], p2.at[y], s5.at[n], r5.at[n], y_dev(n))
                 c.start()
-                ys.append(c)
-        if p == 3:
-            for c in ys:
+                sy.append(c)
+        if p >= 2:
+            for h in PARTS[p - 2]:
+                fold(h)
+        if p == 2:
+            for c in sy:
                 c.wait()
             p3[z] = (p2[0] + p2[1]) + (p2[2] + p2[3])
             zs = []
@@ -476,19 +485,22 @@
                 c = remote(p3.at[z], p3.at[z], s6.at[n], r6.at[n], z_dev(n))
                 c.start()
                 zs.append(c)
-    for p in range(4):
+        if p == 3:
+            for c in zs:
+                c.wait()
+            small[j] = (p3[0] + p3[1]) + (p3[2] + p3[3])
+            fin = []
+            for n in range(1, 8):
+                c = remote(
+                    small.at[j], small.at[j], s7.at[n], r7.at[n], group_peer(seq, x, core, n)
+                )
+                c.start()
+                fin.append(c)
+    for h in PARTS[parts - 2] + PARTS[parts - 1]:
+        fold(h)
+    for p in range(parts):
         for c in direct[p] + passed[p]:
             c.wait_send()
-    fold(6)
-    fold(7)
-    for c in zs:
-        c.wait()
-    small[j] = (p3[0] + p3[1]) + (p3[2] + p3[3])
-    fin = []
-    for n in range(1, 8):
-        c = remote(small.at[j], small.at[j], s7.at[n], r7.at[n], group_peer(seq, x, core, n))
-        c.start()
-        fin.append(c)
     for h in range(8):
         for c in second[h]:
             c.wait()
@@ -505,9 +517,10 @@
         c.wait()
 
 
-def reduce_all(norm, mass, sp, act, pred, live, wo, ft):
+def reduce_all(norm, mass, pre, b_in, wo, bo, live, ft):
     dma = pltpu.SemaphoreType.DMA
     vmem = pl.BlockSpec(memory_space=VM)
+    smem = pl.BlockSpec(memory_space=pltpu.SMEM)
     return pl.pallas_call(
         functools.partial(reduce_kernel, norm),
         name="reduce_all",
@@ -515,11 +528,11 @@
             jax.ShapeDtypeStruct((48, 1024), F32),
             jax.ShapeDtypeStruct((8, 8, 256), F32),
         ),
-        in_specs=[vmem] * 7,
+        in_specs=[vmem, vmem, vmem, vmem, smem, vmem, vmem],
         out_specs=(vmem,) * 2,
         scratch_shapes=[
             VM((4, 8, 128), F32), VM((8, 8, 128), F32), VM((8, 8, 128), F32),
-            VM((4, 8, 128, 256), BF16),
+            VM((8, 8, 128, 128), BF16),
             VM((8, 4, 4, 48, 128), BF16),
             VM((8, 4, 4, 48, 128), F32),
             VM((8, 4, 4, 48, 128), BF16),
@@ -527,13 +540,13 @@
             VM((8, 4, 48, 128), F32),
             VM((8, 8, 256), F32), VM((8, 8, 256), F32), VM((4, 8, 256), F32), VM((4, 8, 256), F32),
         ]
-        + [dma((4,)), dma((4,)), dma((8,)), dma((8,)), dma((32,)), dma((32,)), dma((8,)), dma((8,))]
+        + [dma((4,)), dma((4,)), dma((8,)), dma((8,)), dma((40,)), dma((40,)), dma((8,)), dma((8,))]
         + [dma((4,)), dma((4,)), dma((4,)), dma((4,)), dma((8,)), dma((8,))]
         + [dma((32,)), dma((32,)), dma((32,)), dma((32,))],
         compiler_params=pltpu.CompilerParams(
             collective_id=1, has_side_effects=True, vmem_limit_bytes=40 * 2**20
         ),
-    )(mass, sp, act, pred, live, wo, ft)
+    )(mass, pre, b_in, wo, bo, live, ft)
 
 
 def finish_kernel(g, small, grad, bias, term, last):
@@ -563,11 +576,11 @@
 
 def on_device(queries, keys, values, lengths, block_pos, w_in, b_in, output_weight, output_bias):
     norm = 1.0 / math.sqrt(4 * 4096)
-    qg, kg, ft, sp, act, pred, wot = spread(
-        queries[0], keys[0], values[0], w_in, b_in[None, :], output_weight.T, output_bias
+    qg, kg, ft, pre = spread(queries[0], keys[0], values[0], w_in)
+    mass, live = column_mass(block_pos[0], lengths, qg, kg)
+    g, small = reduce_all(
+        norm, mass.reshape(4, 8, 128), pre, b_in[None, :], output_weight.T, output_bias, live, ft
     )
-    mass, live = column_mass(block_pos[0], lengths, qg, kg)
-    g, small = reduce_all(norm, mass.reshape(4, 8, 128), sp, act, pred, live, wot, ft)
     grad, bias, term, last = finish(g, small)
     return (grad, bias.reshape(1024), term.T, last.reshape(8))
 

time: 104 us -> 99.6 us (0.958)
  local copies, waits for them, and re-layouts: 6.47 us -> 4.43 us
  Pallas kernels: 95.6 us -> 93.9 us
    pallas_call x1, Pallas kernels: 18.1 us -> 14.5 us  [column_mass(): pl.pallas_call(mass_kernel, name='column_mass', out_shape=(jax.ShapeDtype...]
    pallas_call x1, Pallas kernels: 48.1 us -> 50.6 us  [reduce_all(): pl.pallas_call(functools.partial(reduce_kernel, norm), name='reduce_all',...]
    unnamed x18, local copies, waits for them, and re-layouts: 6.47 us -> 4.43 us
where the time goes in v3:
time: 99.6 us; the launch traced here: 99.8 us
  Pallas kernels  93.9 us (94%)
  local copies, waits for them, and re-layouts  4.43 us (4%)
  between operations  1.4 us (1%)
    pallas_call x1, Pallas kernels, reduce_all(): pl.pallas_call(functools.partial(reduce_kernel, norm), name='reduce_all',...  50.6 us
    pallas_call x1, Pallas kernels, spread(): pl.pallas_call(spread_kernel, name='spread', out_shape=(jax.ShapeDtypeStr...  27.2 us
    pallas_call x1, Pallas kernels, column_mass(): pl.pallas_call(mass_kernel, name='column_mass', out_shape=(jax.ShapeDtype...  14.5 us
    unnamed x18, local copies, waits for them, and re-layouts  4.43 us

profile of v3, /device:TPU:1, one launch (start us, length us, event | category | flops | bytes accessed | tf_op | source)
XLA Modules:
  0.0 99.8 jit_solution(10568829728066209440)
XLA Ops:
  0.6 0.0 copy-start.8
  0.6 0.0 copy-start.6
  0.7 0.0 copy-start.7
  1.3 0.0 copy-start
  1.3 1.2 %copy-done = bf16[1,128,4096]{2,1,0:T(8,128)(2,1)S(1)} copy-done((bf16[1,128,4096]{2,1,0:T(8,128)(2,1)S(1)}, bf16[1,128,4096]{2,1,0:T(8,128)(2,1)}, u32[]{:S(2)}) %copy-start) | copy-done | bytes 1048600
  2.6 0.0 copy-start.1
  2.6 0.9 copy-done.1
  3.5 0.0 copy-start.2
  3.5 0.9 copy-done.2
  4.5 0.0 copy-start.5
  4.5 27.2 %spread.1 = (bf16[8,128,512]{2,1,0:T(8,128)(2,1)S(1)}, bf16[32,128,128]{2,1,0:T(8,128)(2,1)S(1)}, bf16[16,48,1024]{2,1,0:T(8,128)(2,1)S(1)}, f32[128,1024]{1,0:T(8,128)S(1)}) custom-call(bf16[128,4096]{1,0:T(8,128)(2,1)S(1)} %bitcast.10, bf16[128,1024]{1,0:T(8,128)(2,1)S(1)} %bitcast.11, bf16[128,1024]{1,0:T(8,128)(2,1)S(1)} %bitcast.12, ...), custom_call_target="tpu_custom_call" | custom-call | tf_op jit(solution)/shard_map/spread/pallas_call | solution.py:198
  31.7 0.0 copy-done.7
  31.7 14.5 %column_mass.1 = (f32[32,128]{1,0:T(8,128)S(1)}, f32[1,128]{1,0:T(1,128)S(1)}) custom-call(s32[32]{0:T(128)S(1)} %bitcast.16, s32[1]{0:T(128)S(6)} %copy.13.length, bf16[8,128,512]{2,1,0:T(8,128)(2,1)S(1)} %get-tuple-element.16.qg, bf16[32,128,128]{2,1,0:T(8,128)(2,1)S(1)} %get-tuple-element.17.kg), custom_call_target="tpu_custom_call" | custom-call | tf_op jit(solution)/shard_map/column_mass/pallas_call | solution.py:304
  46.1 0.0 copy-done.8
  46.2 0.0 copy-done.6
  46.2 0.0 copy-done.5
  46.2 50.6 %reduce_all.1 = (f32[48,1024]{1,0:T(8,128)S(1)}, f32[8,8,256]{2,1,0:T(8,128)S(1)}) custom-call(f32[4,8,128]{2,1,0:T(8,128)S(1)} %bitcast.14, f32[128,1024]{1,0:T(8,128)S(1)} %get-tuple-element.19.pre, f32[1,1024]{1,0:T(1,128)S(1)} %bitcast.15, bf16[8,1024]{1,0:T(8,128)(2,1)S(1)} %bitcast.13, f32[8]{0:T(128)S(1)} %copy-done.8, ...), custom_call_target="tpu_custom_call" | custom-call | tf_op jit(solution)/shard_map/reduce_all/pallas_call | solution.py:524
  96.8 0.0 copy-start.3
  96.8 0.7 copy-done.3
  97.5 0.0 copy-start.4
  97.5 0.6 copy-done.4
  98.1 1.6 %finish.1 = (f32[48,1024]{1,0:T(8,128)}, f32[8,128]{1,0:T(8,128)}, f32[8,1024]{1,0:T(8,128)}, f32[1,8]{1,0:T(1,128)}) custom-call(f32[48,1024]{1,0:T(8,128)} %copy-done.3, f32[8,8,256]{2,1,0:T(8,128)} %copy-done.4), custom_call_target="tpu_custom_call" | custom-call | tf_op jit(solution)/shard_map/finish/pallas_call | solution.py:563
Async XLA Ops:
  0.6 45.5 %copy-start.8 = (f32[8]{0:T(128)S(1)}, f32[8]{0:T(128)}, u32[]{:S(2)}) copy-start(f32[8]{0:T(128)} %bo.1) | copy-start | bytes 100
  0.6 45.5 %copy-start.6 = (f32[1024]{0:T(1024)S(1)}, f32[1024]{0:T(1024)}, u32[]{:S(2)}) copy-start(f32[1024]{0:T(1024)} %param.15) | copy-start | bytes 12292
  0.7 31.0 %copy-start.7 = (s32[1,32]{1,0:T(1,128)S(1)}, s32[1,32]{1,0:T(1,128)}, u32[]{:S(2)}) copy-start(s32[1,32]{1,0:T(1,128)} %param.13) | copy-start | bytes 388
  1.3 1.2 %copy-start = (bf16[1,128,4096]{2,1,0:T(8,128)(2,1)S(1)}, bf16[1,128,4096]{2,1,0:T(8,128)(2,1)}, u32[]{:S(2)}) copy-start(bf16[1,128,4096]{2,1,0:T(8,128)(2,1)} %param.9) | copy-start | bytes 3145732
  2.6 0.9 copy-start.1
  3.5 0.9 copy-start.2
  4.5 41.7 %copy-start.5 = (bf16[1024,8]{0,1:T(8,128)(2,1)S(1)}, bf16[1024,8]{0,1:T(8,128)(2,1)}, u32[]{:S(2)}) copy-start(bf16[1024,8]{0,1:T(8,128)(2,1)} %param.16) | copy-start | bytes 49156
  96.8 0.7 copy-start.3
  97.5 0.6 copy-start.4

commit v4 on v3

--- a/solution.py
+++ b/solution.py
@@ -16,8 +16,8 @@
 WK = 512
 KW = 2
 PARTS = ((0, 1), (2, 3), (4, 5), (6, 7))
-EARLY = 3
-FP = 4
+EARLY = 1
+FP = 1
 
 
 def place():
@@ -59,19 +59,12 @@
 
 
 def spread_kernel(
-    q_hbm, k_hbm, v_hbm, w_hbm, qg, kg, ft_all, pre,
-    q, k, v, ft, wbuf, wsem, isem, ks, kr, qs, qr, fs, fr, ys, yr, ls,
+    q, k, v, w_hbm, qg, kg, ft_all, pre,
+    ft, wbuf, wsem, ks, kr, qs, qr, fs, fr, ys, yr, ls,
 ):
     seq, x, y, row, core = place()
     j = group_rank(x, core)
     chunks = w_hbm.shape[0] // WK
-    ins = [
-        pltpu.make_async_copy(q_hbm, q, isem.at[0]),
-        pltpu.make_async_copy(k_hbm, k, isem.at[1]),
-        pltpu.make_async_copy(v_hbm, v, isem.at[2]),
-    ]
-    for c in ins:
-        c.start()
 
     def fetch(i):
         return pltpu.make_async_copy(
@@ -81,8 +74,6 @@
     fetch(0).start()
     fetch(1).start()
     met = greet(seq, x, y, row, core)
-    for c in ins:
-        c.wait()
     lanes = pl.ds(pl.multiple_of(j * 128, 128), 128)
     kc, qc, fc, yc, own_f = [], [], [], [], []
     span = 16 // FP
@@ -119,14 +110,19 @@
     for part in range(EARLY):
         turn(part)
     met()
-    for n in range(1, 8):
-        to = lax.rem(row + n, 8)
-        c = remote(
-            k.at[:, pl.ds(pl.multiple_of(to * 128, 128), 128)], kg.at[seq],
-            ks.at[n], kr.at[n], (y * 8 + to, x),
-        )
-        c.start()
-        kc.append(c)
+    for n in range(4):
+        cs = []
+        for flip in range(2):
+            if n == 0 and flip == 0:
+                continue
+            to = lax.rem(row // 2 + n, 4) * 2 + lax.rem(core + flip, 2)
+            c = remote(
+                k.at[:, pl.ds(pl.multiple_of(to * 128, 128), 128)], kg.at[seq],
+                ks.at[n * 2 + flip], kr.at[n * 2 + flip], (y * 8 + to, x),
+            )
+            c.start()
+            cs.append(c)
+        kc.append(cs)
     own_k = pltpu.make_async_copy(
         k.at[:, pl.ds(pl.multiple_of(row * 128, 128), 128)], kg.at[seq], ls.at[0]
     )
@@ -164,28 +160,29 @@
         pre[...] = part if i == 0 else pre[...] + part
 
     def pass_on(n):
-        block = kg.at[y * 8 + lax.rem(row + 8 - n, 8)]
-        for m in range(1, 4):
+        pair = kg.at[pl.ds(y * 8 + lax.rem(row // 2 + 4 - n, 4) * 2, 2)]
+        for m in (2, 1, 3):
             c = remote(
-                block, block, ys.at[n * 4 + m], yr.at[n * 4 + m],
+                pair, pair, ys.at[n * 4 + m], yr.at[n * 4 + m],
                 (lax.rem(y + m, 4) * 8 + row, x),
             )
             c.start()
             yc.append(c)
 
     own_k.wait()
-    pass_on(0)
-    for i in range(KW):
-        multiply(i)
-    for n in range(1, 8):
-        kc[n - 1].wait_recv()
+    for n in range(4):
+        for c in kc[n]:
+            c.wait_recv()
         pass_on(n)
+        if n < KW:
+            multiply(n)
     for i in range(KW, chunks):
         multiply(i)
     for c in qc + fc + yc:
         c.wait()
-    for c in kc:
-        c.wait_send()
+    for cs in kc:
+        for c in cs:
+            c.wait_send()
     own_q.wait()
     for c in own_f:
         c.wait()
@@ -204,17 +201,14 @@
             jax.ShapeDtypeStruct((16, 48, 1024), BF16),
             jax.ShapeDtypeStruct((128, 1024), F32),
         ),
-        in_specs=[hbm, hbm, hbm, hbm],
+        in_specs=[vmem, vmem, vmem, hbm],
         out_specs=(vmem,) * 4,
         scratch_shapes=[
-            VM((128, 4096), BF16),
-            VM((128, 1024), BF16),
-            VM((128, 1024), BF16),
             VM((16, 8, 48, 128), BF16),
             VM((3, WK, 1024), BF16),
-            dma((3,)), dma((3,)),
+            dma((3,)),
             dma((8,)), dma((8,)), dma((8,)), dma((8,)),
-            dma((8 * FP,)), dma((8 * FP,)), dma((32,)), dma((32,)),
+            dma((8 * FP,)), dma((8 * FP,)), dma((16,)), dma((16,)),
             dma((2 + FP,)),
         ],
         compiler_params=pltpu.CompilerParams(
@@ -571,6 +565,7 @@
         ),
         in_specs=[vmem] * 2,
         out_specs=(vmem,) * 4,
+        compiler_params=pltpu.CompilerParams(vmem_limit_bytes=8 * 2**20),
     )(g, small)
 
 

time: 99.6 us -> 98.5 us (0.989)
  local copies, waits for them, and re-layouts: 4.43 us -> 3.13 us
    pallas_call x1, Pallas kernels: 50.6 us -> 55.5 us  [reduce_all(): pl.pallas_call(functools.partial(reduce_kernel, norm), name='reduce_all',...]
    pallas_call x1, Pallas kernels: 14.5 us -> 10.8 us  [column_mass(): pl.pallas_call(mass_kernel, name='column_mass', out_shape=(jax.ShapeDtype...]
    unnamed x18 -> x14, local copies, waits for them, and re-layouts: 4.43 us -> 3.13 us
where the time goes in v4:
time: 98.5 us; the launch traced here: 97.8 us
  Pallas kernels  93.2 us (95%)
  local copies, waits for them, and re-layouts  3.13 us (3%)
  between operations  1.39 us (1%)
    pallas_call x1, Pallas kernels, reduce_all(): pl.pallas_call(functools.partial(reduce_kernel, norm), name='reduce_all',...  55.5 us
    pallas_call x1, Pallas kernels, spread(): pl.pallas_call(spread_kernel, name='spread', out_shape=(jax.ShapeDtypeStr...  26.2 us
    pallas_call x1, Pallas kernels, column_mass(): pl.pallas_call(mass_kernel, name='column_mass', out_shape=(jax.ShapeDtype...  10.8 us
    unnamed x14, local copies, waits for them, and re-layouts  3.13 us

profile of v4, /device:TPU:1, one launch (start us, length us, event | category | flops | bytes accessed | tf_op | source)
XLA Modules:
  0.0 97.8 jit_solution(517924949816631167)
XLA Ops:
  0.6 0.0 copy-start.6
  0.6 0.0 copy-start.4
  0.7 0.0 copy-start.5
  1.3 0.0 copy-start
  1.3 1.2 %copy-done = bf16[1,128,4096]{2,1,0:T(8,128)(2,1)S(1)} copy-done((bf16[1,128,4096]{2,1,0:T(8,128)(2,1)S(1)}, bf16[1,128,4096]{2,1,0:T(8,128)(2,1)}, u32[]{:S(2)}) %copy-start) | copy-done | bytes 1048600
  2.6 0.0 copy-start.1
  2.6 0.9 copy-done.1
  3.5 0.0 copy-start.2
  3.5 0.9 copy-done.2
  4.5 0.0 copy-start.3
  4.5 26.2 %spread.1 = (bf16[8,128,512]{2,1,0:T(8,128)(2,1)S(1)}, bf16[32,128,128]{2,1,0:T(8,128)(2,1)S(1)}, bf16[16,48,1024]{2,1,0:T(8,128)(2,1)S(1)}, f32[128,1024]{1,0:T(8,128)S(1)}) custom-call(bf16[128,4096]{1,0:T(8,128)(2,1)S(1)} %bitcast.10, bf16[128,1024]{1,0:T(8,128)(2,1)S(1)} %bitcast.11, bf16[128,1024]{1,0:T(8,128)(2,1)S(1)} %bitcast.12, ...), custom_call_target="tpu_custom_call" | custom-call | tf_op jit(solution)/shard_map/spread/pallas_call | solution.py:195
  30.7 0.0 copy-done.5
  30.7 10.8 %column_mass.1 = (f32[32,128]{1,0:T(8,128)S(1)}, f32[1,128]{1,0:T(1,128)S(1)}) custom-call(s32[32]{0:T(128)S(1)} %bitcast.16, s32[1]{0:T(128)S(6)} %copy.13.length, bf16[8,128,512]{2,1,0:T(8,128)(2,1)S(1)} %get-tuple-element.16.qg, bf16[32,128,128]{2,1,0:T(8,128)(2,1)S(1)} %get-tuple-element.17.kg), custom_call_target="tpu_custom_call" | custom-call | tf_op jit(solution)/shard_map/column_mass/pallas_call | solution.py:298
  41.5 0.0 copy-done.6
  41.5 0.0 copy-done.4
  41.5 0.0 copy-done.3
  41.5 55.5 %reduce_all.1 = (f32[48,1024]{1,0:T(8,128)S(1)}, f32[8,8,256]{2,1,0:T(8,128)S(1)}) custom-call(f32[4,8,128]{2,1,0:T(8,128)S(1)} %bitcast.14, f32[128,1024]{1,0:T(8,128)S(1)} %get-tuple-element.19.pre, f32[1,1024]{1,0:T(1,128)S(1)} %bitcast.15, bf16[8,1024]{1,0:T(8,128)(2,1)S(1)} %bitcast.13, f32[8]{0:T(128)S(1)} %copy-done.6, ...), custom_call_target="tpu_custom_call" | custom-call | tf_op jit(solution)/shard_map/reduce_all/pallas_call | solution.py:518
  97.1 0.7 finish.1
Async XLA Ops:
  0.6 40.9 %copy-start.6 = (f32[8]{0:T(128)S(1)}, f32[8]{0:T(128)}, u32[]{:S(2)}) copy-start(f32[8]{0:T(128)} %bo.1) | copy-start | bytes 100
  0.6 40.9 %copy-start.4 = (f32[1024]{0:T(1024)S(1)}, f32[1024]{0:T(1024)}, u32[]{:S(2)}) copy-start(f32[1024]{0:T(1024)} %param.15) | copy-start | bytes 12292
  0.7 30.0 %copy-start.5 = (s32[1,32]{1,0:T(1,128)S(1)}, s32[1,32]{1,0:T(1,128)}, u32[]{:S(2)}) copy-start(s32[1,32]{1,0:T(1,128)} %param.13) | copy-start | bytes 388
  1.3 1.2 %copy-start = (bf16[1,128,4096]{2,1,0:T(8,128)(2,1)S(1)}, bf16[1,128,4096]{2,1,0:T(8,128)(2,1)}, u32[]{:S(2)}) copy-start(bf16[1,128,4096]{2,1,0:T(8,128)(2,1)} %param.9) | copy-start | bytes 3145732
  2.6 0.9 copy-start.1
  3.5 0.9 copy-start.2
  4.5 37.1 %copy-start.3 = (bf16[1024,8]{0,1:T(8,128)(2,1)S(1)}, bf16[1024,8]{0,1:T(8,128)(2,1)}, u32[]{:S(2)}) copy-start(bf16[1024,8]{0,1:T(8,128)(2,1)} %param.16) | copy-start | bytes 49156

commit v5 on v4

--- a/solution.py
+++ b/solution.py
@@ -226,10 +226,11 @@
     factor = math.log2(math.e) / math.sqrt(128)
 
     def order(r, _):
-        kpos[pl.ds(pl.multiple_of(meta[r] * 128, 128), 128)] = kg[r]
+        for t in range(8):
+            kpos[pl.ds(pl.multiple_of(meta[r * 8 + t] * 128, 128), 128)] = kg[r * 8 + t]
         return 0
 
-    lax.fori_loop(0, 32, order, 0)
+    lax.fori_loop(0, 4, order, 0)
     acc[...] = jnp.zeros_like(acc)
     lane = lax.rem(lax.broadcasted_iota(jnp.int32, (1, 512), 1), 128)
     sub = lax.broadcasted_iota(jnp.int32, (CK, 512), 0)
@@ -285,11 +286,12 @@
     lax.fori_loop(0, 8, block, 0)
 
     def give(r, _):
-        rows = acc[pl.ds(pl.multiple_of(meta[r] * 128, 128), 128)]
-        out[pl.ds(r, 1)] = jnp.sum(rows.T, axis=0, keepdims=True)
+        for t in range(16):
+            rows = acc[pl.ds(pl.multiple_of(meta[r * 16 + t] * 128, 128), 128)]
+            out[pl.ds(r * 16 + t, 1)] = jnp.sum(rows.T, axis=0, keepdims=True)
         return 0
 
-    lax.fori_loop(0, 32, give, 0)
+    lax.fori_loop(0, 2, give, 0)
 
 
 def column_mass(order, length, qg, kg):
@@ -412,7 +414,7 @@
                 t = t + rs[h, lax.rem(z + n, 4)].astype(F32)
         ps[h] = t
         cs = []
-        for n in range(1, 4):
+        for n in (2, 1, 3):
             if h % 2 == 0:
                 c = remote(
                     ps.at[h, lax.rem(z + n, 4)], ts.at[h, z],
@@ -432,6 +434,9 @@
         for c, d in zip(direct[p], passed[p][1:]):
             c.wait_recv()
             d.start()
+        if p >= 2:
+            for h in PARTS[p - 2]:
+                fold(h)
         for c in passed[p]:
             c.wait_recv()
         d_all = jnp.concatenate([dl[h].reshape(1024, 128) for h in PARTS[p]], axis=1)
@@ -441,7 +446,7 @@
             gs[h] = half.astype(BF16)
             res[h] = half
             cs = []
-            for n in range(1, 4):
+            for n in (2, 1, 3):
                 if h % 2 == 0:
                     c = remote(
                         gs.at[h, lax.rem(y + n, 4)], rs.at[h, y],
@@ -467,9 +472,6 @@
                 c = remote(p2.at[y], p2.at[y], s5.at[n], r5.at[n], y_dev(n))
                 c.start()
                 sy.append(c)
-        if p >= 2:
-            for h in PARTS[p - 2]:
-                fold(h)
         if p == 2:
             for c in sy:
                 c.wait()

time: 98.5 us -> 94.5 us (0.959)
  Pallas kernels: 93.2 us -> 89.2 us
    pallas_call x1, Pallas kernels: 10.8 us -> 7.4 us  [column_mass(): pl.pallas_call(mass_kernel, name='column_mass', out_shape=(jax.ShapeDtype...]
where the time goes in v5:
time: 94.5 us; the launch traced here: 93.7 us
  Pallas kernels  89.2 us (94%)
  local copies, waits for them, and re-layouts  3.13 us (3%)
  between operations  1.39 us (1%)
    pallas_call x1, Pallas kernels, reduce_all(): pl.pallas_call(functools.partial(reduce_kernel, norm), name='reduce_all',...  54.9 us
    pallas_call x1, Pallas kernels, spread(): pl.pallas_call(spread_kernel, name='spread', out_shape=(jax.ShapeDtypeStr...  26.2 us
    pallas_call x1, Pallas kernels, column_mass(): pl.pallas_call(mass_kernel, name='column_mass', out_shape=(jax.ShapeDtype...  7.4 us
    unnamed x14, local copies, waits for them, and re-layouts  3.13 us

profile of v5, /device:TPU:1, one launch (start us, length us, event | category | flops | bytes accessed | tf_op | source)
XLA Modules:
  0.0 93.7 jit_solution(5553092637204724198)
XLA Ops:
  0.6 0.0 copy-start.6
  0.6 0.0 copy-start.4
  0.7 0.0 copy-start.5
  1.3 0.0 copy-start
  1.3 1.2 %copy-done = bf16[1,128,4096]{2,1,0:T(8,128)(2,1)S(1)} copy-done((bf16[1,128,4096]{2,1,0:T(8,128)(2,1)S(1)}, bf16[1,128,4096]{2,1,0:T(8,128)(2,1)}, u32[]{:S(2)}) %copy-start) | copy-done | bytes 1048600
  2.6 0.0 copy-start.1
  2.6 0.9 %copy-done.1 = bf16[1,128,1024]{2,1,0:T(8,128)(2,1)S(1)} copy-done((bf16[1,128,1024]{2,1,0:T(8,128)(2,1)S(1)}, bf16[1,128,1024]{2,1,0:T(8,128)(2,1)}, u32[]{:S(2)}) %copy-start.1) | copy-done | bytes 262168
  3.5 0.0 copy-start.2
  3.5 0.9 %copy-done.2 = bf16[1,128,1024]{2,1,0:T(8,128)(2,1)S(1)} copy-done((bf16[1,128,1024]{2,1,0:T(8,128)(2,1)S(1)}, bf16[1,128,1024]{2,1,0:T(8,128)(2,1)}, u32[]{:S(2)}) %copy-start.2) | copy-done | bytes 262168
  4.5 0.0 copy-start.3
  4.5 26.2 %spread.1 = (bf16[8,128,512]{2,1,0:T(8,128)(2,1)S(1)}, bf16[32,128,128]{2,1,0:T(8,128)(2,1)S(1)}, bf16[16,48,1024]{2,1,0:T(8,128)(2,1)S(1)}, f32[128,1024]{1,0:T(8,128)S(1)}) custom-call(bf16[128,4096]{1,0:T(8,128)(2,1)S(1)} %bitcast.10, bf16[128,1024]{1,0:T(8,128)(2,1)S(1)} %bitcast.11, bf16[128,1024]{1,0:T(8,128)(2,1)S(1)} %bitcast.12, ...), custom_call_target="tpu_custom_call" | custom-call | tf_op jit(solution)/shard_map/spread/pallas_call | solution.py:195
  30.7 0.0 copy-done.5
  30.7 7.4 %column_mass.1 = (f32[32,128]{1,0:T(8,128)S(1)}, f32[1,128]{1,0:T(1,128)S(1)}) custom-call(s32[32]{0:T(128)S(1)} %bitcast.16, s32[1]{0:T(128)S(6)} %copy.13.length, bf16[8,128,512]{2,1,0:T(8,128)(2,1)S(1)} %get-tuple-element.16.qg, bf16[32,128,128]{2,1,0:T(8,128)(2,1)S(1)} %get-tuple-element.17.kg), custom_call_target="tpu_custom_call" | custom-call | tf_op jit(solution)/shard_map/column_mass/pallas_call | solution.py:300
  38.1 0.0 copy-done.6
  38.1 0.0 copy-done.4
  38.1 0.0 copy-done.3
  38.1 54.9 %reduce_all.1 = (f32[48,1024]{1,0:T(8,128)S(1)}, f32[8,8,256]{2,1,0:T(8,128)S(1)}) custom-call(f32[4,8,128]{2,1,0:T(8,128)S(1)} %bitcast.14, f32[128,1024]{1,0:T(8,128)S(1)} %get-tuple-element.19.pre, f32[1,1024]{1,0:T(1,128)S(1)} %bitcast.15, bf16[8,1024]{1,0:T(8,128)(2,1)S(1)} %bitcast.13, f32[8]{0:T(128)S(1)} %copy-done.6, ...), custom_call_target="tpu_custom_call" | custom-call | tf_op jit(solution)/shard_map/reduce_all/pallas_call | solution.py:520
  93.0 0.7 finish.1
Async XLA Ops:
  0.6 37.5 %copy-start.6 = (f32[8]{0:T(128)S(1)}, f32[8]{0:T(128)}, u32[]{:S(2)}) copy-start(f32[8]{0:T(128)} %bo.1) | copy-start | bytes 100
  0.6 37.5 %copy-start.4 = (f32[1024]{0:T(1024)S(1)}, f32[1024]{0:T(1024)}, u32[]{:S(2)}) copy-start(f32[1024]{0:T(1024)} %param.15) | copy-start | bytes 12292
  0.7 30.0 %copy-start.5 = (s32[1,32]{1,0:T(1,128)S(1)}, s32[1,32]{1,0:T(1,128)}, u32[]{:S(2)}) copy-start(s32[1,32]{1,0:T(1,128)} %param.13) | copy-start | bytes 388
  1.3 1.2 %copy-start = (bf16[1,128,4096]{2,1,0:T(8,128)(2,1)S(1)}, bf16[1,128,4096]{2,1,0:T(8,128)(2,1)}, u32[]{:S(2)}) copy-start(bf16[1,128,4096]{2,1,0:T(8,128)(2,1)} %param.9) | copy-start | bytes 3145732
  2.6 0.9 %copy-start.1 = (bf16[1,128,1024]{2,1,0:T(8,128)(2,1)S(1)}, bf16[1,128,1024]{2,1,0:T(8,128)(2,1)}, u32[]{:S(2)}) copy-start(bf16[1,128,1024]{2,1,0:T(8,128)(2,1)} %param.10) | copy-start | bytes 786436
  3.5 0.9 %copy-start.2 = (bf16[1,128,1024]{2,1,0:T(8,128)(2,1)S(1)}, bf16[1,128,1024]{2,1,0:T(8,128)(2,1)}, u32[]{:S(2)}) copy-start(bf16[1,128,1024]{2,1,0:T(8,128)(2,1)} %param.11) | copy-start | bytes 786436
  4.5 33.7 %copy-start.3 = (bf16[1024,8]{0,1:T(8,128)(2,1)S(1)}, bf16[1024,8]{0,1:T(8,128)(2,1)}, u32[]{:S(2)}) copy-start(bf16[1024,8]{0,1:T(8,128)(2,1)} %param.16) | copy-start | bytes 49156

commit v6 on v5

--- a/solution.py
+++ b/solution.py
@@ -12,7 +12,7 @@
 F32 = jnp.float32
 BF16 = jnp.bfloat16
 VM = pltpu.VMEM
-CK = 512
+CK = 1024
 WK = 512
 KW = 2
 PARTS = ((0, 1), (2, 3), (4, 5), (6, 7))

time: 94.5 us -> 93.6 us (level)
    pallas_call x1, Pallas kernels: 54.9 us -> 40.8 us  [reduce_all(): pl.pallas_call(functools.partial(reduce_kernel, norm), name='reduce_all',...]
    pallas_call x1, Pallas kernels: 7.4 us -> 20.6 us  [column_mass(): pl.pallas_call(mass_kernel, name='column_mass', out_shape=(jax.ShapeDtype...]
where the time goes in v6:
time: 93.6 us; the launch traced here: 92.8 us
  Pallas kernels  88.3 us (94%)
  local copies, waits for them, and re-layouts  3.13 us (3%)
  between operations  1.39 us (1%)
    pallas_call x1, Pallas kernels, reduce_all(): pl.pallas_call(functools.partial(reduce_kernel, norm), name='reduce_all',...  40.8 us
    pallas_call x1, Pallas kernels, spread(): pl.pallas_call(spread_kernel, name='spread', out_shape=(jax.ShapeDtypeStr...  26.2 us
    pallas_call x1, Pallas kernels, column_mass(): pl.pallas_call(mass_kernel, name='column_mass', out_shape=(jax.ShapeDtype...  20.6 us
    unnamed x14, local copies, waits for them, and re-layouts  3.13 us

profile of v6, /device:TPU:1, one launch (start us, length us, event | category | flops | bytes accessed | tf_op | source)
XLA Modules:
  0.0 92.8 jit_solution(4596255655096923034)
XLA Ops:
  0.6 0.0 copy-start.6
  0.6 0.0 copy-start.4
  0.7 0.0 copy-start.5
  1.3 0.0 copy-start
  1.3 1.2 %copy-done = bf16[1,128,4096]{2,1,0:T(8,128)(2,1)S(1)} copy-done((bf16[1,128,4096]{2,1,0:T(8,128)(2,1)S(1)}, bf16[1,128,4096]{2,1,0:T(8,128)(2,1)}, u32[]{:S(2)}) %copy-start) | copy-done | bytes 1048600
  2.6 0.0 copy-start.1
  2.6 0.9 %copy-done.1 = bf16[1,128,1024]{2,1,0:T(8,128)(2,1)S(1)} copy-done((bf16[1,128,1024]{2,1,0:T(8,128)(2,1)S(1)}, bf16[1,128,1024]{2,1,0:T(8,128)(2,1)}, u32[]{:S(2)}) %copy-start.1) | copy-done | bytes 262168
  3.5 0.0 copy-start.2
  3.5 0.9 %copy-done.2 = bf16[1,128,1024]{2,1,0:T(8,128)(2,1)S(1)} copy-done((bf16[1,128,1024]{2,1,0:T(8,128)(2,1)S(1)}, bf16[1,128,1024]{2,1,0:T(8,128)(2,1)}, u32[]{:S(2)}) %copy-start.2) | copy-done | bytes 262168
  4.5 0.0 copy-start.3
  4.5 26.2 %spread.1 = (bf16[8,128,512]{2,1,0:T(8,128)(2,1)S(1)}, bf16[32,128,128]{2,1,0:T(8,128)(2,1)S(1)}, bf16[16,48,1024]{2,1,0:T(8,128)(2,1)S(1)}, f32[128,1024]{1,0:T(8,128)S(1)}) custom-call(bf16[128,4096]{1,0:T(8,128)(2,1)S(1)} %bitcast.10, bf16[128,1024]{1,0:T(8,128)(2,1)S(1)} %bitcast.11, bf16[128,1024]{1,0:T(8,128)(2,1)S(1)} %bitcast.12, ...), custom_call_target="tpu_custom_call" | custom-call | tf_op jit(solution)/shard_map/spread/pallas_call | solution.py:195
  30.7 0.0 copy-done.5
  30.7 20.6 %column_mass.1 = (f32[32,128]{1,0:T(8,128)S(1)}, f32[1,128]{1,0:T(1,128)S(1)}) custom-call(s32[32]{0:T(128)S(1)} %bitcast.16, s32[1]{0:T(128)S(6)} %copy.13.length, bf16[8,128,512]{2,1,0:T(8,128)(2,1)S(1)} %get-tuple-element.16.qg, bf16[32,128,128]{2,1,0:T(8,128)(2,1)S(1)} %get-tuple-element.17.kg), custom_call_target="tpu_custom_call" | custom-call | tf_op jit(solution)/shard_map/column_mass/pallas_call | solution.py:300
  51.3 0.0 copy-done.6
  51.3 0.0 copy-done.4
  51.3 0.0 copy-done.3
  51.3 40.8 %reduce_all.1 = (f32[48,1024]{1,0:T(8,128)S(1)}, f32[8,8,256]{2,1,0:T(8,128)S(1)}) custom-call(f32[4,8,128]{2,1,0:T(8,128)S(1)} %bitcast.14, f32[128,1024]{1,0:T(8,128)S(1)} %get-tuple-element.19.pre, f32[1,1024]{1,0:T(1,128)S(1)} %bitcast.15, bf16[8,1024]{1,0:T(8,128)(2,1)S(1)} %bitcast.13, f32[8]{0:T(128)S(1)} %copy-done.6, ...), custom_call_target="tpu_custom_call" | custom-call | tf_op jit(solution)/shard_map/reduce_all/pallas_call | solution.py:520
  92.1 0.7 finish.1
Async XLA Ops:
  0.6 50.7 %copy-start.6 = (f32[8]{0:T(128)S(1)}, f32[8]{0:T(128)}, u32[]{:S(2)}) copy-start(f32[8]{0:T(128)} %bo.1) | copy-start | bytes 100
  0.6 50.7 %copy-start.4 = (f32[1024]{0:T(1024)S(1)}, f32[1024]{0:T(1024)}, u32[]{:S(2)}) copy-start(f32[1024]{0:T(1024)} %param.15) | copy-start | bytes 12292
  0.7 30.0 %copy-start.5 = (s32[1,32]{1,0:T(1,128)S(1)}, s32[1,32]{1,0:T(1,128)}, u32[]{:S(2)}) copy-start(s32[1,32]{1,0:T(1,128)} %param.13) | copy-start | bytes 388
  1.3 1.2 %copy-start = (bf16[1,128,4096]{2,1,0:T(8,128)(2,1)S(1)}, bf16[1,128,4096]{2,1,0:T(8,128)(2,1)}, u32[]{:S(2)}) copy-start(bf16[1,128,4096]{2,1,0:T(8,128)(2,1)} %param.9) | copy-start | bytes 3145732
  2.6 0.9 %copy-start.1 = (bf16[1,128,1024]{2,1,0:T(8,128)(2,1)S(1)}, bf16[1,128,1024]{2,1,0:T(8,128)(2,1)}, u32[]{:S(2)}) copy-start(bf16[1,128,1024]{2,1,0:T(8,128)(2,1)} %param.10) | copy-start | bytes 786436
  3.5 0.9 %copy-start.2 = (bf16[1,128,1024]{2,1,0:T(8,128)(2,1)S(1)}, bf16[1,128,1024]{2,1,0:T(8,128)(2,1)}, u32[]{:S(2)}) copy-start(bf16[1,128,1024]{2,1,0:T(8,128)(2,1)} %param.11) | copy-start | bytes 786436
  4.5 46.9 %copy-start.3 = (bf16[1024,8]{0,1:T(8,128)(2,1)S(1)}, bf16[1024,8]{0,1:T(8,128)(2,1)}, u32[]{:S(2)}) copy-start(bf16[1024,8]{0,1:T(8,128)(2,1)} %param.16) | copy-start | bytes 49156

commit v7 on v6

--- a/solution.py
+++ b/solution.py
@@ -236,7 +236,7 @@
     sub = lax.broadcasted_iota(jnp.int32, (CK, 512), 0)
 
     def fold(a, op):
-        return op(a.reshape(CK // 8, 8, 512), axis=0)
+        return op(a.reshape(a.shape[0] // 8, 8, 512), axis=0)
 
     def block(i, _):
         pos = meta[first + i]
@@ -244,42 +244,54 @@
         @pl.when(pos * 128 < limit)
         def _():
             last = pos * 128 // CK
+            big = lax.rem(pos, CK // 128) // (CK // 256)
             q4 = jnp.concatenate([qg[i, :, h * 128 : (h + 1) * 128] for h in range(4)], axis=0)
 
-            def scores(c):
-                rows = pl.ds(pl.multiple_of(c * CK, CK), CK)
-                return rows, lax.dot_general(
+            def span(size, c):
+                return pl.ds(pl.multiple_of(c * CK, CK), size)
+
+            def first_pass(size, masked, c, top):
+                rows = span(size, c)
+                s = lax.dot_general(
                     kpos[rows], q4, (((1,), (1,)), ((), ())), preferred_element_type=F32
                 )
-
-            def first_pass(c, top):
-                rows, s = scores(c)
+                if masked:
+                    s = jnp.where(sub[0:size] <= lane + (pos * 128 - c * CK), s, -1e30)
                 s_ref[rows] = s
                 return jnp.maximum(top, fold(s, jnp.max))
 
-            top = lax.fori_loop(0, last, first_pass, jnp.full((8, 512), -1e30, F32))
-            rows, s = scores(last)
-            s = jnp.where(sub + last * CK <= lane + pos * 128, s, -1e30)
-            s_ref[rows] = s
-            top = jnp.max(jnp.maximum(top, fold(s, jnp.max)), axis=0, keepdims=True)
-
-            def second_pass(c, total):
-                rows = pl.ds(pl.multiple_of(c * CK, CK), CK)
+            def run(step, state):
+                state = lax.fori_loop(0, last + big, functools.partial(step, CK), state)
+                return lax.fori_loop(
+                    last + big, last + 1, functools.partial(step, CK // 2), state
+                )
+
+            top = jnp.full((8, 512), -1e30, F32)
+            top = lax.fori_loop(0, last, functools.partial(first_pass, CK, False), top)
+            top = lax.fori_loop(
+                last, last + big, functools.partial(first_pass, CK, True), top
+            )
+            top = lax.fori_loop(
+                last + big, last + 1, functools.partial(first_pass, CK // 2, True), top
+            )
+            top = jnp.max(top, axis=0, keepdims=True)
+
+            def second_pass(size, c, total):
+                rows = span(size, c)
                 e = jnp.exp2((s_ref[rows] - top) * factor)
                 s_ref[rows] = e
                 return total + fold(e, jnp.sum)
 
-            total = lax.fori_loop(0, last + 1, second_pass, jnp.zeros((8, 512), F32))
-            total = jnp.sum(total, axis=0, keepdims=True)
+            total = jnp.sum(run(second_pass, jnp.zeros((8, 512), F32)), axis=0, keepdims=True)
             share = jnp.where(lane + pos * 128 < limit, 1.0 / total, 0.0)
 
-            def third_pass(c, _):
-                rows = pl.ds(pl.multiple_of(c * CK, CK), CK)
+            def third_pass(size, c, _):
+                rows = span(size, c)
                 e = s_ref[rows] * share
                 acc[rows] += (e[:, 0:128] + e[:, 128:256]) + (e[:, 256:384] + e[:, 384:512])
                 return 0
 
-            lax.fori_loop(0, last + 1, third_pass, 0)
+            run(third_pass, 0)
 
         return 0
 

time: 93.6 us -> 91.6 us (0.979)
  Pallas kernels: 88.3 us -> 86.9 us
where the time goes in v7:
time: 91.6 us; the launch traced here: 91.4 us
  Pallas kernels  86.9 us (95%)
  local copies, waits for them, and re-layouts  3.13 us (3%)
  between operations  1.39 us (2%)
    pallas_call x1, Pallas kernels, reduce_all(): pl.pallas_call(functools.partial(reduce_kernel, norm), name='reduce_all',...  40 us
    pallas_call x1, Pallas kernels, spread(): pl.pallas_call(spread_kernel, name='spread', out_shape=(jax.ShapeDtypeStr...  26.2 us
    pallas_call x1, Pallas kernels, column_mass(): pl.pallas_call(mass_kernel, name='column_mass', out_shape=(jax.ShapeDtype...  20 us
    unnamed x14, local copies, waits for them, and re-layouts  3.13 us

profile of v7, /device:TPU:1, one launch (start us, length us, event | category | flops | bytes accessed | tf_op | source)
XLA Modules:
  0.0 91.4 jit_solution(5918017478828397453)
XLA Ops:
  0.6 0.0 copy-start.6
  0.6 0.0 copy-start.4
  0.7 0.0 copy-start.5
  1.3 0.0 copy-start
  1.3 1.2 %copy-done = bf16[1,128,4096]{2,1,0:T(8,128)(2,1)S(1)} copy-done((bf16[1,128,4096]{2,1,0:T(8,128)(2,1)S(1)}, bf16[1,128,4096]{2,1,0:T(8,128)(2,1)}, u32[]{:S(2)}) %copy-start) | copy-done | bytes 1048600
  2.6 0.0 copy-start.1
  2.6 0.9 %copy-done.1 = bf16[1,128,1024]{2,1,0:T(8,128)(2,1)S(1)} copy-done((bf16[1,128,1024]{2,1,0:T(8,128)(2,1)S(1)}, bf16[1,128,1024]{2,1,0:T(8,128)(2,1)}, u32[]{:S(2)}) %copy-start.1) | copy-done | bytes 262168
  3.5 0.0 copy-start.2
  3.5 0.9 %copy-done.2 = bf16[1,128,1024]{2,1,0:T(8,128)(2,1)S(1)} copy-done((bf16[1,128,1024]{2,1,0:T(8,128)(2,1)S(1)}, bf16[1,128,1024]{2,1,0:T(8,128)(2,1)}, u32[]{:S(2)}) %copy-start.2) | copy-done | bytes 262168
  4.5 0.0 copy-start.3
  4.5 26.2 %spread.1 = (bf16[8,128,512]{2,1,0:T(8,128)(2,1)S(1)}, bf16[32,128,128]{2,1,0:T(8,128)(2,1)S(1)}, bf16[16,48,1024]{2,1,0:T(8,128)(2,1)S(1)}, f32[128,1024]{1,0:T(8,128)S(1)}) custom-call(bf16[128,4096]{1,0:T(8,128)(2,1)S(1)} %bitcast.10, bf16[128,1024]{1,0:T(8,128)(2,1)S(1)} %bitcast.11, bf16[128,1024]{1,0:T(8,128)(2,1)S(1)} %bitcast.12, ...), custom_call_target="tpu_custom_call" | custom-call | tf_op jit(solution)/shard_map/spread/pallas_call | solution.py:195
  30.7 0.0 copy-done.5
  30.7 20.0 %column_mass.1 = (f32[32,128]{1,0:T(8,128)S(1)}, f32[1,128]{1,0:T(1,128)S(1)}) custom-call(s32[32]{0:T(128)S(1)} %bitcast.16, s32[1]{0:T(128)S(6)} %copy.13.length, bf16[8,128,512]{2,1,0:T(8,128)(2,1)S(1)} %get-tuple-element.16.qg, bf16[32,128,128]{2,1,0:T(8,128)(2,1)S(1)} %get-tuple-element.17.kg), custom_call_target="tpu_custom_call" | custom-call | tf_op jit(solution)/shard_map/column_mass/pallas_call | solution.py:312
  50.7 0.0 copy-done.6
  50.7 0.0 copy-done.4
  50.7 0.0 copy-done.3
  50.7 40.0 %reduce_all.1 = (f32[48,1024]{1,0:T(8,128)S(1)}, f32[8,8,256]{2,1,0:T(8,128)S(1)}) custom-call(f32[4,8,128]{2,1,0:T(8,128)S(1)} %bitcast.14, f32[128,1024]{1,0:T(8,128)S(1)} %get-tuple-element.19.pre, f32[1,1024]{1,0:T(1,128)S(1)} %bitcast.15, bf16[8,1024]{1,0:T(8,128)(2,1)S(1)} %bitcast.13, f32[8]{0:T(128)S(1)} %copy-done.6, ...), custom_call_target="tpu_custom_call" | custom-call | tf_op jit(solution)/shard_map/reduce_all/pallas_call | solution.py:532
  90.7 0.7 finish.1
Async XLA Ops:
  0.6 50.1 %copy-start.6 = (f32[8]{0:T(128)S(1)}, f32[8]{0:T(128)}, u32[]{:S(2)}) copy-start(f32[8]{0:T(128)} %bo.1) | copy-start | bytes 100
  0.6 50.1 %copy-start.4 = (f32[1024]{0:T(1024)S(1)}, f32[1024]{0:T(1024)}, u32[]{:S(2)}) copy-start(f32[1024]{0:T(1024)} %param.15) | copy-start | bytes 12292
  0.7 30.0 %copy-start.5 = (s32[1,32]{1,0:T(1,128)S(1)}, s32[1,32]{1,0:T(1,128)}, u32[]{:S(2)}) copy-start(s32[1,32]{1,0:T(1,128)} %param.13) | copy-start | bytes 388
  1.3 1.2 %copy-start = (bf16[1,128,4096]{2,1,0:T(8,128)(2,1)S(1)}, bf16[1,128,4096]{2,1,0:T(8,128)(2,1)}, u32[]{:S(2)}) copy-start(bf16[1,128,4096]{2,1,0:T(8,128)(2,1)} %param.9) | copy-start | bytes 3145732
  2.6 0.9 %copy-start.1 = (bf16[1,128,1024]{2,1,0:T(8,128)(2,1)S(1)}, bf16[1,128,1024]{2,1,0:T(8,128)(2,1)}, u32[]{:S(2)}) copy-start(bf16[1,128,1024]{2,1,0:T(8,128)(2,1)} %param.10) | copy-start | bytes 786436
  3.5 0.9 %copy-start.2 = (bf16[1,128,1024]{2,1,0:T(8,128)(2,1)S(1)}, bf16[1,128,1024]{2,1,0:T(8,128)(2,1)}, u32[]{:S(2)}) copy-start(bf16[1,128,1024]{2,1,0:T(8,128)(2,1)} %param.11) | copy-start | bytes 786436
  4.5 46.3 %copy-start.3 = (bf16[1024,8]{0,1:T(8,128)(2,1)S(1)}, bf16[1024,8]{0,1:T(8,128)(2,1)}, u32[]{:S(2)}) copy-start(bf16[1024,8]{0,1:T(8,128)(2,1)} %param.16) | copy-start | bytes 49156
